TPU v7x, 128 devices: a whole 4x4x4 slice. The times are simulated.
128 devices in a mesh: dp: 1, tp: 16 (over z, y), cp: 8 (over x, core).
Axes of the slice: x: 4, y: 4, z: 4, core: 2. Of those that a mesh axis runs over, the one named last changes fastest.
Arguments:
- x_in: bfloat16 [16384, 3072], P(('dp', 'cp', 'tp'))
- seg_ids: int32 [16384], P(('dp', 'cp', 'tp'))
- w_q: bfloat16 [3072, 16, 256], P(None, 'tp')
- w_k: bfloat16 [3072, 16, 256], P(None, 'tp')
- w_v: bfloat16 [3072, 16, 256], P(None, 'tp')
- w_o: bfloat16 [16, 256, 3072], P('tp')
Outputs:
- output: bfloat16 [16384, 3072], P(('dp', 'cp', 'tp'))
All inputs are finite; a program needn't handle non-finite values.
Results may differ from a plain program's by a relative error of at most 0.00482496.
Values are sent between devices in bfloat16 or wider.
A program may use at most 1 GiB of HBM per device.

v0:
```python
import jax
import jax.numpy as jnp
from jax import lax
from jax.sharding import PartitionSpec as P

NEG_BIG = -1e30


def block_update(softmax_state, q_blk, k_blk, v_blk, allowed, logit_scale):
    m_old, l_old, acc_old = softmax_state
    scores = jnp.einsum("qkge,ske->kgqs", q_blk, k_blk, preferred_element_type=jnp.float32) * logit_scale
    scores = jnp.where(allowed, scores, NEG_BIG)
    m_new = jnp.maximum(m_old, jnp.max(scores, axis=-1))
    prob_blk = jnp.exp(scores - m_new[..., None])
    rescale = jnp.exp(m_old - m_new)
    pv_part = jnp.einsum("kgqs,ske->kgqe", prob_blk.astype(jnp.bfloat16), v_blk, preferred_element_type=jnp.float32)
    return m_new, rescale * l_old + jnp.sum(prob_blk, axis=-1), rescale[..., None] * acc_old + pv_part


def visible_mask(pos_q, seg_q, pos_k, seg_k):
    return (seg_q[:, None] == seg_k[None, :]) & (pos_k[None, :] <= pos_q[:, None])


def solution(mesh):
    n_cp = mesh.shape["cp"]
    next_perm = [(dev_idx, (dev_idx + 1) % n_cp) for dev_idx in range(n_cp)]

    def per_device(x_loc, seg_loc, w_q, w_k, w_v, w_o):
        cp_rank = lax.axis_index("cp")
        x_rows = lax.all_gather(x_loc, "tp", axis=0, tiled=True)
        seg_rows = lax.all_gather(seg_loc, "tp", axis=0, tiled=True)
        n_rows = x_rows.shape[0]
        piece_len = n_rows // 2
        kv_loc = w_k.shape[1]
        head_dim = w_k.shape[2]
        q_per_kv = w_q.shape[1] // kv_loc
        logit_scale = head_dim ** -0.5
        q_rows = jnp.einsum("sd,dhe->she", x_rows, w_q, preferred_element_type=jnp.float32).astype(jnp.bfloat16).reshape(n_rows, kv_loc, q_per_kv, head_dim)
        k_rows = jnp.einsum("sd,dhe->she", x_rows, w_k, preferred_element_type=jnp.float32).astype(jnp.bfloat16)
        v_rows = jnp.einsum("sd,dhe->she", x_rows, w_v, preferred_element_type=jnp.float32).astype(jnp.bfloat16)
        local_idx = jnp.arange(n_rows)

        def piece_positions(owner_rank):
            return jnp.where(local_idx < piece_len, owner_rank * piece_len + local_idx, (2 * n_cp - 1 - owner_rank) * piece_len + local_idx - piece_len)

        pos_q = piece_positions(cp_rank)
        late_q = q_rows[piece_len:]
        late_pos = pos_q[piece_len:]
        late_seg = seg_rows[piece_len:]
        state_shape = (kv_loc, q_per_kv, n_rows)
        init_state = (jnp.full(state_shape, NEG_BIG, jnp.float32), jnp.zeros(state_shape, jnp.float32), jnp.zeros(state_shape + (head_dim,), jnp.float32))
        first_state = block_update(init_state, q_rows, k_rows, v_rows, visible_mask(pos_q, seg_rows, pos_q, seg_rows), logit_scale)

        def kv_step(step_idx, loop_carry):
            k_cur, v_cur, seg_cur, softmax_state = loop_carry
            k_cur = lax.ppermute(k_cur, "cp", next_perm)
            v_cur = lax.ppermute(v_cur, "cp", next_perm)
            seg_cur = lax.ppermute(seg_cur, "cp", next_perm)
            src_rank = (cp_rank - step_idx) % n_cp
            pos_k = piece_positions(src_rank)

            def from_earlier(old_state):
                return block_update(old_state, q_rows, k_cur[:piece_len], v_cur[:piece_len], visible_mask(pos_q, seg_rows, pos_k[:piece_len], seg_cur[:piece_len]), logit_scale)

            def from_later(old_state):
                m_old, l_old, acc_old = old_state
                late_state = block_update((m_old[..., piece_len:], l_old[..., piece_len:], acc_old[:, :, piece_len:]), late_q, k_cur, v_cur, visible_mask(late_pos, late_seg, pos_k, seg_cur), logit_scale)
                return (jnp.concatenate([m_old[..., :piece_len], late_state[0]], axis=-1),
                        jnp.concatenate([l_old[..., :piece_len], late_state[1]], axis=-1),
                        jnp.concatenate([acc_old[:, :, :piece_len], late_state[2]], axis=2))

            new_state = lax.cond(src_rank < cp_rank, from_earlier, from_later, softmax_state)
            return k_cur, v_cur, seg_cur, new_state

        final_carry = lax.fori_loop(1, n_cp, kv_step, (k_rows, v_rows, seg_rows, first_state))
        l_fin = final_carry[3][1]
        acc_fin = final_carry[3][2]
        attn_out = (acc_fin / l_fin[..., None]).astype(jnp.bfloat16)
        y_part = jnp.einsum("kgqe,kged->qd", attn_out, w_o.reshape(kv_loc, q_per_kv, head_dim, -1), preferred_element_type=jnp.float32)
        return lax.psum_scatter(y_part, "tp", scatter_dimension=0, tiled=True).astype(jnp.bfloat16)

    return jax.shard_map(
        per_device,
        mesh=mesh,
        in_specs=(P(("dp", "cp", "tp"), None), P(("dp", "cp", "tp")), P(None, "tp", None), P(None, "tp", None), P(None, "tp", None), P("tp", None, None)),
        out_specs=P(("dp", "cp", "tp"), None),
        check_vma=False,
    )
```

profile of v0, /device:TPU:1, one launch (start us, length us, event | category | flops | bytes accessed | tf_op | source)
XLA Modules:
  0.0 607.1 jit_solution(14774261908479830514)
XLA Ops:
  7.3 20.8 %all-gather = s32[16,1,128]{2,1,0:T(1,128)S(1)} all-gather(s32[1,1,128]{2,1,0:T(1,128)} %bitcast.125), channel_id=1, replica_groups=mesh['dp'=1,'tp'=16,'cp'=8] {'tp'}, dimensions={0}, use_global_device_ids=true | all-gather | bytes 8704 | tf_op jit(solution)/shard_map/all_gather | solution.py:31
  28.2 74.1 %all-gather.3.cloned.1.call-done = bf16[2048,3072]{1,0:T(8,128)(2,1)} async-done(((bf16[128,3072]{1,0:T(8,128)(2,1)}), bf16[2048,3072]{1,0:T(8,128)(2,1)}) %all-gather.3.cloned.1.call-update) | async-done | bytes 12582928 | tf_op jit(solution)/shard_map/all_gather | solution.py:30
  102.3 9.6 %convolution_convert_fusion = bf16[2048,256]{1,0:T(8,128)(2,1)} fusion(bf16[2048,3072]{1,0:T(8,128)(2,1)} %all-gather.3.cloned.1.call-done, bf16[3072,1,256]{2,0,1:T(8,128)(2,1)} %param.12), kind=kOutput, calls=%fused_computation.52 | convolution fusion | flops 3221749760 | bytes 15204352 | tf_op jit(solution)/shard_map/sd,dhe->she/dot_general | solution.py:38
  113.1 3.7 convolution_convert_fusion.2
  116.8 9.1 %fusion.59 = (f32[2048]{0:T(1024)S(1)}, f32[1,1,2048,2048]{2,3,1,0:T(8,128)}) fusion(bf16[2048,256]{1,0:T(8,128)(2,1)S(1)} %convolution_convert_fusion.2, bf16[2048,256]{1,0:T(8,128)(2,1)} %convolution_convert_fusion, s32[2048]{0:T(1024)S(1)} %add_select_fusion, s32[2048]{0:T(1024)S(1)} %bitcast.121), kind=kOutput, calls=%fused_computation.70 | convolution fusion | flops 2172647424 | bytes 18898944 | tf_op jit(solution)/shard_map/qkge,ske->kgqs/dot_general | solution.py:11
  125.9 8.2 %fusion.40 = f32[2048]{0:T(1024)S(1)} fusion(f32[1,1,2048,2048]{2,3,1,0:T(8,128)} %get-tuple-element.593, f32[2048]{0:T(1024)S(1)} %get-tuple-element.591), kind=kLoop, calls=%fused_computation.46 | loop fusion | flops 8386560 | bytes 16793600 | tf_op jit(solution)/shard_map/reduce_sum | solution.py:17
  134.2 6.7 %convolution_convert_fusion.1 = bf16[2048,256]{1,0:T(8,128)(2,1)S(1)} fusion(bf16[2048,3072]{1,0:T(8,128)(2,1)} %all-gather.3.cloned.1.call-done, bf16[3072,1,256]{2,0,1:T(8,128)(2,1)S(1)} %copy-done.7), kind=kOutput, calls=%fused_computation.53 | convolution fusion | flops 3221749760 | bytes 15204352 | tf_op jit(solution)/shard_map/sd,dhe->she/dot_general | solution.py:40
  140.8 3.1 copy-done.4
  143.9 3.8 fusion.48
  147.7 280.2 %while.27 = (s32[]{:T(128)}, bf16[2048,1,256]{2,0,1:T(8,128)(2,1)}, bf16[2048,1,256]{2,0,1:T(8,128)(2,1)}, s32[2048]{0:T(1024)S(1)}, f32[1,1,2048]{2,1,0:T(1,128...) while((s32[]{:T(128)}, bf16[2048,1,256]{2,0,1:T(8,128)(2,1)}, ...), condition=%wide.region_9.10_spmd.clone.clone, body=%wide.region_2.9_spmd.clone.clone.sunk | while | flops 2169528320 | bytes 61100820 | solution.py:75
  151.5 21.5 %collective-permute-done.2 = s32[2048]{0:T(1024)S(1)} collective-permute-done((s32[2048]{0:T(1024)S(1)}, s32[2048]{0:T(1024)S(1)}, u32[]{:S(2)}, u32[]{:S(2)}) %collective-permute-start.2) | collective-permute-done | bytes 8224 | tf_op jit(solution)/shard_map/while/body/eval_jaxpr/ppermute | solution.py:58
  173.0 11.0 %conditional.4 = (f32[1,1,2048]{2,1,0:T(1,128)}, f32[1,1,2048]{2,1,0:T(1,128)S(1)}, f32[1,1,2048,256]{3,2,1,0:T(8,128)}) conditional(s32[]{:T(128)} %convert_element_type.83, (f32[1,1,2048]{2,1,0:T(1,128)S(1)}, s32[1024]{0:T(1024)S(1)}, s32[2048]{0:T(1024)S(1)}, s32[2048]{0:T(1024)S(1)}, s32[1024]{0:T(1024)S(1)}, ...), branch_computations={%region_3.5_spmd, %region_6.8_spmd} | conditional | flops 2169516032 | bytes 48425048 | solution.py:72
  173.1 3.4 fusion.58
  179.8 2.9 fusion.28
  185.7 2.3 copy.32
  188.0 2.5 collective-permute-start.1
  192.1 21.5 %collective-permute-done.2 = s32[2048]{0:T(1024)S(1)} collective-permute-done((s32[2048]{0:T(1024)S(1)}, s32[2048]{0:T(1024)S(1)}, u32[]{:S(2)}, u32[]{:S(2)}) %collective-permute-start.2) | collective-permute-done | bytes 8224 | tf_op jit(solution)/shard_map/while/body/eval_jaxpr/ppermute | solution.py:58
  213.6 10.3 %conditional.4 = (f32[1,1,2048]{2,1,0:T(1,128)}, f32[1,1,2048]{2,1,0:T(1,128)S(1)}, f32[1,1,2048,256]{3,2,1,0:T(8,128)}) conditional(s32[]{:T(128)} %convert_element_type.83, (f32[1,1,2048]{2,1,0:T(1,128)S(1)}, s32[1024]{0:T(1024)S(1)}, s32[2048]{0:T(1024)S(1)}, s32[2048]{0:T(1024)S(1)}, s32[1024]{0:T(1024)S(1)}, ...), branch_computations={%region_3.5_spmd, %region_6.8_spmd} | conditional | flops 2169516032 | bytes 48425048 | solution.py:72
  214.9 3.9 fusion.57
  225.6 2.3 copy.32
  227.9 3.2 collective-permute-start.1
  232.7 21.5 %collective-permute-done.2 = s32[2048]{0:T(1024)S(1)} collective-permute-done((s32[2048]{0:T(1024)S(1)}, s32[2048]{0:T(1024)S(1)}, u32[]{:S(2)}, u32[]{:S(2)}) %collective-permute-start.2) | collective-permute-done | bytes 8224 | tf_op jit(solution)/shard_map/while/body/eval_jaxpr/ppermute | solution.py:58
  254.2 10.3 %conditional.4 = (f32[1,1,2048]{2,1,0:T(1,128)}, f32[1,1,2048]{2,1,0:T(1,128)S(1)}, f32[1,1,2048,256]{3,2,1,0:T(8,128)}) conditional(s32[]{:T(128)} %convert_element_type.83, (f32[1,1,2048]{2,1,0:T(1,128)S(1)}, s32[1024]{0:T(1024)S(1)}, s32[2048]{0:T(1024)S(1)}, s32[2048]{0:T(1024)S(1)}, s32[1024]{0:T(1024)S(1)}, ...), branch_computations={%region_3.5_spmd, %region_6.8_spmd} | conditional | flops 2169516032 | bytes 48425048 | solution.py:72
  255.5 3.9 fusion.57
  268.4 2.5 collective-permute-start.1
  273.2 20.8 %collective-permute-done.2 = s32[2048]{0:T(1024)S(1)} collective-permute-done((s32[2048]{0:T(1024)S(1)}, s32[2048]{0:T(1024)S(1)}, u32[]{:S(2)}, u32[]{:S(2)}) %collective-permute-start.2) | collective-permute-done | bytes 8224 | tf_op jit(solution)/shard_map/while/body/eval_jaxpr/ppermute | solution.py:58
  294.0 10.3 %conditional.4 = (f32[1,1,2048]{2,1,0:T(1,128)}, f32[1,1,2048]{2,1,0:T(1,128)S(1)}, f32[1,1,2048,256]{3,2,1,0:T(8,128)}) conditional(s32[]{:T(128)} %convert_element_type.83, (f32[1,1,2048]{2,1,0:T(1,128)S(1)}, s32[1024]{0:T(1024)S(1)}, s32[2048]{0:T(1024)S(1)}, s32[2048]{0:T(1024)S(1)}, s32[1024]{0:T(1024)S(1)}, ...), branch_computations={%region_3.5_spmd, %region_6.8_spmd} | conditional | flops 2169516032 | bytes 48425048 | solution.py:72
  295.3 3.9 fusion.57
  308.3 2.5 collective-permute-start.1
  310.8 3.0 collective-permute-start.2
  313.8 20.1 %collective-permute-done.2 = s32[2048]{0:T(1024)S(1)} collective-permute-done((s32[2048]{0:T(1024)S(1)}, s32[2048]{0:T(1024)S(1)}, u32[]{:S(2)}, u32[]{:S(2)}) %collective-permute-start.2) | collective-permute-done | bytes 8224 | tf_op jit(solution)/shard_map/while/body/eval_jaxpr/ppermute | solution.py:58
  333.9 10.3 %conditional.4 = (f32[1,1,2048]{2,1,0:T(1,128)}, f32[1,1,2048]{2,1,0:T(1,128)S(1)}, f32[1,1,2048,256]{3,2,1,0:T(8,128)}) conditional(s32[]{:T(128)} %convert_element_type.83, (f32[1,1,2048]{2,1,0:T(1,128)S(1)}, s32[1024]{0:T(1024)S(1)}, s32[2048]{0:T(1024)S(1)}, s32[2048]{0:T(1024)S(1)}, s32[1024]{0:T(1024)S(1)}, ...), branch_computations={%region_3.5_spmd, %region_6.8_spmd} | conditional | flops 2169516032 | bytes 48425048 | solution.py:72
  335.2 3.9 fusion.57
  345.9 2.3 copy.32
  348.2 2.5 collective-permute-start.1
  351.2 2.5 collective-permute-start.2
  353.7 20.1 %collective-permute-done.2 = s32[2048]{0:T(1024)S(1)} collective-permute-done((s32[2048]{0:T(1024)S(1)}, s32[2048]{0:T(1024)S(1)}, u32[]{:S(2)}, u32[]{:S(2)}) %collective-permute-start.2) | collective-permute-done | bytes 8224 | tf_op jit(solution)/shard_map/while/body/eval_jaxpr/ppermute | solution.py:58
  373.8 10.3 %conditional.4 = (f32[1,1,2048]{2,1,0:T(1,128)}, f32[1,1,2048]{2,1,0:T(1,128)S(1)}, f32[1,1,2048,256]{3,2,1,0:T(8,128)}) conditional(s32[]{:T(128)} %convert_element_type.83, (f32[1,1,2048]{2,1,0:T(1,128)S(1)}, s32[1024]{0:T(1024)S(1)}, s32[2048]{0:T(1024)S(1)}, s32[2048]{0:T(1024)S(1)}, s32[1024]{0:T(1024)S(1)}, ...), branch_computations={%region_3.5_spmd, %region_6.8_spmd} | conditional | flops 2169516032 | bytes 48425048 | solution.py:72
  375.1 3.9 fusion.57
  385.8 2.3 copy.32
  388.1 2.5 collective-permute-start.1
  391.0 2.5 collective-permute-start.2
  393.6 20.1 %collective-permute-done.2 = s32[2048]{0:T(1024)S(1)} collective-permute-done((s32[2048]{0:T(1024)S(1)}, s32[2048]{0:T(1024)S(1)}, u32[]{:S(2)}, u32[]{:S(2)}) %collective-permute-start.2) | collective-permute-done | bytes 8224 | tf_op jit(solution)/shard_map/while/body/eval_jaxpr/ppermute | solution.py:58
  413.6 10.3 %conditional.4 = (f32[1,1,2048]{2,1,0:T(1,128)}, f32[1,1,2048]{2,1,0:T(1,128)S(1)}, f32[1,1,2048,256]{3,2,1,0:T(8,128)}) conditional(s32[]{:T(128)} %convert_element_type.83, (f32[1,1,2048]{2,1,0:T(1,128)S(1)}, s32[1024]{0:T(1024)S(1)}, s32[2048]{0:T(1024)S(1)}, s32[2048]{0:T(1024)S(1)}, s32[1024]{0:T(1024)S(1)}, ...), branch_computations={%region_3.5_spmd, %region_6.8_spmd} | conditional | flops 2169516032 | bytes 48425048 | solution.py:72
  415.0 3.9 fusion.57
  427.9 11.8 %fusion.51 = f32[2048,3072]{1,0:T(8,128)} fusion(bf16[1,256,3072]{2,1,0:T(8,128)(2,1)S(1)} %copy-done, f32[1,1,2048,256]{3,2,1,0:T(8,128)} %get-tuple-element.444, f32[2048]{0:T(1024)S(1)} %bitcast.114), kind=kOutput, calls=%fused_computation.56 | convolution fusion | flops 3222274048 | bytes 28844032 | tf_op jit(solution)/shard_map/kgqe,kged->qd/dot_general | solution.py:79
  439.7 158.1 %reduce-scatter.2.cloned.1.call-done = f32[128,3072]{1,0:T(8,128)} async-done(((f32[2048,3072]{1,0:T(8,128)}), f32[128,3072]{1,0:T(8,128)}) %reduce-scatter.2.cloned.1.call-update) | async-done | bytes 1572880 | tf_op jit(solution)/shard_map/reduce_scatter | solution.py:80
  597.9 2.4 convert_element_type.48
  (166 shorter events, 73.4 us)
Async XLA Ops:
  6.5 421.4 %copy-start = (bf16[1,256,3072]{2,1,0:T(8,128)(2,1)S(1)}, bf16[1,256,3072]{2,1,0:T(8,128)(2,1)}, u32[]{:S(2)}) copy-start(bf16[1,256,3072]{2,1,0:T(8,128)(2,1)} %param.15) | copy-start | bytes 4718596
  6.5 95.8 %all-gather.3.cloned.1.call-start = ((), (), s32[]{:S(2)}) async-start(), calls=%async_computation.1 | async-start | bytes 13369344 | tf_op jit(solution)/shard_map/all_gather | solution.py:30
  7.3 590.6 %reduce-scatter.2.cloned.1.call-start = ((), (), s32[]{:S(2)}) async-start(), calls=%async_computation.2 | async-start | bytes 26738688 | tf_op jit(solution)/shard_map/reduce_scatter | solution.py:80
  102.3 10.7 %copy-start.5 = (bf16[2048,3072]{1,0:T(8,128)(2,1)S(1)}, bf16[2048,3072]{1,0:T(8,128)(2,1)}, u32[]{:S(2)}) copy-start(bf16[2048,3072]{1,0:T(8,128)(2,1)} %all-gather.3.cloned.1.call-done) | copy-start | bytes 37748740
  102.3 10.7 %copy-start.6 = (bf16[3072,1,256]{2,0,1:T(8,128)(2,1)S(1)}, bf16[3072,1,256]{2,0,1:T(8,128)(2,1)}, u32[]{:S(2)}) copy-start(bf16[3072,1,256]{2,0,1:T(8,128)(2,1)} %param.13) | copy-start | bytes 4718596
  116.8 9.2 %copy-start.8 = (bf16[2048,256]{1,0:T(8,128)(2,1)}, bf16[2048,256]{1,0:T(8,128)(2,1)S(1)}, u32[]{:S(2)}) copy-start(bf16[2048,256]{1,0:T(8,128)(2,1)S(1)} %convolution_convert_fusion.2) | copy-start | bytes 3145732
  125.9 8.2 %copy-start.7 = (bf16[3072,1,256]{2,0,1:T(8,128)(2,1)S(1)}, bf16[3072,1,256]{2,0,1:T(8,128)(2,1)}, u32[]{:S(2)}) copy-start(bf16[3072,1,256]{2,0,1:T(8,128)(2,1)} %param.14) | copy-start | bytes 4718596
  134.1 9.8 %copy-start.4 = (f32[1,1,2048,2048]{2,3,1,0:T(8,128)S(1)}, f32[1,1,2048,2048]{2,3,1,0:T(8,128)}, u32[]{:S(2)}) copy-start(f32[1,1,2048,2048]{2,3,1,0:T(8,128)} %get-tuple-element.593) | copy-start | bytes 50331652
  140.8 6.8 %copy-start.9 = (bf16[2048,256]{1,0:T(8,128)(2,1)}, bf16[2048,256]{1,0:T(8,128)(2,1)S(1)}, u32[]{:S(2)}) copy-start(bf16[2048,256]{1,0:T(8,128)(2,1)S(1)} %convolution_convert_fusion.1) | copy-start | bytes 3145732
  147.9 25.1 %collective-permute-start.1 = (bf16[2048,1,256]{2,0,1:T(8,128)(2,1)}, bf16[2048,1,256]{2,0,1:T(8,128)(2,1)S(1)}, u32[]{:S(2)}, u32[]{:S(2)}) collective-permute-start(bf16[2048,1,256]{2,0,1:T(8,128)(2,1)} %get-tuple-element.721), channel_id=1, source_target_pairs={{0,1},{1,2},{2,3},{3,4},{4,5},{5,6},{6,7},{7,0},{8,9},{9,10},{10,1... | collective-permute-start | bytes 3145736 | tf_op jit(solution)/shard_map/while/body/eval_jaxpr/ppermute | solution.py:57
  149.9 23.1 %collective-permute-start = (bf16[2048,1,256]{2,0,1:T(8,128)(2,1)}, bf16[2048,1,256]{2,0,1:T(8,128)(2,1)}, u32[]{:S(2)}, u32[]{:S(2)}) collective-permute-start(bf16[2048,1,256]{2,0,1:T(8,128)(2,1)} %get-tuple-element.720), channel_id=1, source_target_pairs={{0,1},{1,2},{2,3},{3,4},{4,5},{5,6},{6,7},{7,0},{8,9},{9,10},{10,1... | collective-permute-start | bytes 3145736 | tf_op jit(solution)/shard_map/while/body/eval_jaxpr/ppermute | solution.py:56
  150.0 23.0 %collective-permute-start.2 = (s32[2048]{0:T(1024)S(1)}, s32[2048]{0:T(1024)S(1)}, u32[]{:S(2)}, u32[]{:S(2)}) collective-permute-start(s32[2048]{0:T(1024)S(1)} %get-tuple-element.722), channel_id=1, source_target_pairs={{0,1},{1,2},{2,3},{3,4},{4,5},{5,6},{6,7},{7,0},{8,9},{9,10},{10,1... | collective-permute-start | bytes 24584 | tf_op jit(solution)/shard_map/while/body/eval_jaxpr/ppermute | solution.py:58
  176.5 3.3 copy-start.2
  182.7 1.4 copy-start.3
  188.0 25.6 %collective-permute-start.1 = (bf16[2048,1,256]{2,0,1:T(8,128)(2,1)}, bf16[2048,1,256]{2,0,1:T(8,128)(2,1)S(1)}, u32[]{:S(2)}, u32[]{:S(2)}) collective-permute-start(bf16[2048,1,256]{2,0,1:T(8,128)(2,1)} %get-tuple-element.721), channel_id=1, source_target_pairs={{0,1},{1,2},{2,3},{3,4},{4,5},{5,6},{6,7},{7,0},{8,9},{9,10},{10,1... | collective-permute-start | bytes 3145736 | tf_op jit(solution)/shard_map/while/body/eval_jaxpr/ppermute | solution.py:57
  190.5 23.1 %collective-permute-start = (bf16[2048,1,256]{2,0,1:T(8,128)(2,1)}, bf16[2048,1,256]{2,0,1:T(8,128)(2,1)}, u32[]{:S(2)}, u32[]{:S(2)}) collective-permute-start(bf16[2048,1,256]{2,0,1:T(8,128)(2,1)} %get-tuple-element.720), channel_id=1, source_target_pairs={{0,1},{1,2},{2,3},{3,4},{4,5},{5,6},{6,7},{7,0},{8,9},{9,10},{10,1... | collective-permute-start | bytes 3145736 | tf_op jit(solution)/shard_map/while/body/eval_jaxpr/ppermute | solution.py:56
  190.5 23.0 %collective-permute-start.2 = (s32[2048]{0:T(1024)S(1)}, s32[2048]{0:T(1024)S(1)}, u32[]{:S(2)}, u32[]{:S(2)}) collective-permute-start(s32[2048]{0:T(1024)S(1)} %get-tuple-element.722), channel_id=1, source_target_pairs={{0,1},{1,2},{2,3},{3,4},{4,5},{5,6},{6,7},{7,0},{8,9},{9,10},{10,1... | collective-permute-start | bytes 24584 | tf_op jit(solution)/shard_map/while/body/eval_jaxpr/ppermute | solution.py:58
  218.8 1.6 copy-start.1
  227.9 26.3 %collective-permute-start.1 = (bf16[2048,1,256]{2,0,1:T(8,128)(2,1)}, bf16[2048,1,256]{2,0,1:T(8,128)(2,1)S(1)}, u32[]{:S(2)}, u32[]{:S(2)}) collective-permute-start(bf16[2048,1,256]{2,0,1:T(8,128)(2,1)} %get-tuple-element.721), channel_id=1, source_target_pairs={{0,1},{1,2},{2,3},{3,4},{4,5},{5,6},{6,7},{7,0},{8,9},{9,10},{10,1... | collective-permute-start | bytes 3145736 | tf_op jit(solution)/shard_map/while/body/eval_jaxpr/ppermute | solution.py:57
  231.1 23.1 %collective-permute-start = (bf16[2048,1,256]{2,0,1:T(8,128)(2,1)}, bf16[2048,1,256]{2,0,1:T(8,128)(2,1)}, u32[]{:S(2)}, u32[]{:S(2)}) collective-permute-start(bf16[2048,1,256]{2,0,1:T(8,128)(2,1)} %get-tuple-element.720), channel_id=1, source_target_pairs={{0,1},{1,2},{2,3},{3,4},{4,5},{5,6},{6,7},{7,0},{8,9},{9,10},{10,1... | collective-permute-start | bytes 3145736 | tf_op jit(solution)/shard_map/while/body/eval_jaxpr/ppermute | solution.py:56
  231.1 23.0 %collective-permute-start.2 = (s32[2048]{0:T(1024)S(1)}, s32[2048]{0:T(1024)S(1)}, u32[]{:S(2)}, u32[]{:S(2)}) collective-permute-start(s32[2048]{0:T(1024)S(1)} %get-tuple-element.722), channel_id=1, source_target_pairs={{0,1},{1,2},{2,3},{3,4},{4,5},{5,6},{6,7},{7,0},{8,9},{9,10},{10,1... | collective-permute-start | bytes 24584 | tf_op jit(solution)/shard_map/while/body/eval_jaxpr/ppermute | solution.py:58
  259.4 1.6 copy-start.1
  268.4 25.6 %collective-permute-start.1 = (bf16[2048,1,256]{2,0,1:T(8,128)(2,1)}, bf16[2048,1,256]{2,0,1:T(8,128)(2,1)S(1)}, u32[]{:S(2)}, u32[]{:S(2)}) collective-permute-start(bf16[2048,1,256]{2,0,1:T(8,128)(2,1)} %get-tuple-element.721), channel_id=1, source_target_pairs={{0,1},{1,2},{2,3},{3,4},{4,5},{5,6},{6,7},{7,0},{8,9},{9,10},{10,1... | collective-permute-start | bytes 3145736 | tf_op jit(solution)/shard_map/while/body/eval_jaxpr/ppermute | solution.py:57
  271.0 23.1 %collective-permute-start = (bf16[2048,1,256]{2,0,1:T(8,128)(2,1)}, bf16[2048,1,256]{2,0,1:T(8,128)(2,1)}, u32[]{:S(2)}, u32[]{:S(2)}) collective-permute-start(bf16[2048,1,256]{2,0,1:T(8,128)(2,1)} %get-tuple-element.720), channel_id=1, source_target_pairs={{0,1},{1,2},{2,3},{3,4},{4,5},{5,6},{6,7},{7,0},{8,9},{9,10},{10,1... | collective-permute-start | bytes 3145736 | tf_op jit(solution)/shard_map/while/body/eval_jaxpr/ppermute | solution.py:56
  271.0 23.0 %collective-permute-start.2 = (s32[2048]{0:T(1024)S(1)}, s32[2048]{0:T(1024)S(1)}, u32[]{:S(2)}, u32[]{:S(2)}) collective-permute-start(s32[2048]{0:T(1024)S(1)} %get-tuple-element.722), channel_id=1, source_target_pairs={{0,1},{1,2},{2,3},{3,4},{4,5},{5,6},{6,7},{7,0},{8,9},{9,10},{10,1... | collective-permute-start | bytes 24584 | tf_op jit(solution)/shard_map/while/body/eval_jaxpr/ppermute | solution.py:58
  299.3 1.6 copy-start.1
  308.3 25.6 %collective-permute-start.1 = (bf16[2048,1,256]{2,0,1:T(8,128)(2,1)}, bf16[2048,1,256]{2,0,1:T(8,128)(2,1)S(1)}, u32[]{:S(2)}, u32[]{:S(2)}) collective-permute-start(bf16[2048,1,256]{2,0,1:T(8,128)(2,1)} %get-tuple-element.721), channel_id=1, source_target_pairs={{0,1},{1,2},{2,3},{3,4},{4,5},{5,6},{6,7},{7,0},{8,9},{9,10},{10,1... | collective-permute-start | bytes 3145736 | tf_op jit(solution)/shard_map/while/body/eval_jaxpr/ppermute | solution.py:57
  310.8 23.1 %collective-permute-start = (bf16[2048,1,256]{2,0,1:T(8,128)(2,1)}, bf16[2048,1,256]{2,0,1:T(8,128)(2,1)}, u32[]{:S(2)}, u32[]{:S(2)}) collective-permute-start(bf16[2048,1,256]{2,0,1:T(8,128)(2,1)} %get-tuple-element.720), channel_id=1, source_target_pairs={{0,1},{1,2},{2,3},{3,4},{4,5},{5,6},{6,7},{7,0},{8,9},{9,10},{10,1... | collective-permute-start | bytes 3145736 | tf_op jit(solution)/shard_map/while/body/eval_jaxpr/ppermute | solution.py:56
  310.8 23.0 %collective-permute-start.2 = (s32[2048]{0:T(1024)S(1)}, s32[2048]{0:T(1024)S(1)}, u32[]{:S(2)}, u32[]{:S(2)}) collective-permute-start(s32[2048]{0:T(1024)S(1)} %get-tuple-element.722), channel_id=1, source_target_pairs={{0,1},{1,2},{2,3},{3,4},{4,5},{5,6},{6,7},{7,0},{8,9},{9,10},{10,1... | collective-permute-start | bytes 24584 | tf_op jit(solution)/shard_map/while/body/eval_jaxpr/ppermute | solution.py:58
  339.1 1.6 copy-start.1
  348.2 25.6 %collective-permute-start.1 = (bf16[2048,1,256]{2,0,1:T(8,128)(2,1)}, bf16[2048,1,256]{2,0,1:T(8,128)(2,1)S(1)}, u32[]{:S(2)}, u32[]{:S(2)}) collective-permute-start(bf16[2048,1,256]{2,0,1:T(8,128)(2,1)} %get-tuple-element.721), channel_id=1, source_target_pairs={{0,1},{1,2},{2,3},{3,4},{4,5},{5,6},{6,7},{7,0},{8,9},{9,10},{10,1... | collective-permute-start | bytes 3145736 | tf_op jit(solution)/shard_map/while/body/eval_jaxpr/ppermute | solution.py:57
  350.7 23.1 %collective-permute-start = (bf16[2048,1,256]{2,0,1:T(8,128)(2,1)}, bf16[2048,1,256]{2,0,1:T(8,128)(2,1)}, u32[]{:S(2)}, u32[]{:S(2)}) collective-permute-start(bf16[2048,1,256]{2,0,1:T(8,128)(2,1)} %get-tuple-element.720), channel_id=1, source_target_pairs={{0,1},{1,2},{2,3},{3,4},{4,5},{5,6},{6,7},{7,0},{8,9},{9,10},{10,1... | collective-permute-start | bytes 3145736 | tf_op jit(solution)/shard_map/while/body/eval_jaxpr/ppermute | solution.py:56
  351.2 22.6 %collective-permute-start.2 = (s32[2048]{0:T(1024)S(1)}, s32[2048]{0:T(1024)S(1)}, u32[]{:S(2)}, u32[]{:S(2)}) collective-permute-start(s32[2048]{0:T(1024)S(1)} %get-tuple-element.722), channel_id=1, source_target_pairs={{0,1},{1,2},{2,3},{3,4},{4,5},{5,6},{6,7},{7,0},{8,9},{9,10},{10,1... | collective-permute-start | bytes 24584 | tf_op jit(solution)/shard_map/while/body/eval_jaxpr/ppermute | solution.py:58
  379.0 1.6 copy-start.1
  388.1 25.6 %collective-permute-start.1 = (bf16[2048,1,256]{2,0,1:T(8,128)(2,1)}, bf16[2048,1,256]{2,0,1:T(8,128)(2,1)S(1)}, u32[]{:S(2)}, u32[]{:S(2)}) collective-permute-start(bf16[2048,1,256]{2,0,1:T(8,128)(2,1)} %get-tuple-element.721), channel_id=1, source_target_pairs={{0,1},{1,2},{2,3},{3,4},{4,5},{5,6},{6,7},{7,0},{8,9},{9,10},{10,1... | collective-permute-start | bytes 3145736 | tf_op jit(solution)/shard_map/while/body/eval_jaxpr/ppermute | solution.py:57
  390.6 23.1 %collective-permute-start = (bf16[2048,1,256]{2,0,1:T(8,128)(2,1)}, bf16[2048,1,256]{2,0,1:T(8,128)(2,1)}, u32[]{:S(2)}, u32[]{:S(2)}) collective-permute-start(bf16[2048,1,256]{2,0,1:T(8,128)(2,1)} %get-tuple-element.720), channel_id=1, source_target_pairs={{0,1},{1,2},{2,3},{3,4},{4,5},{5,6},{6,7},{7,0},{8,9},{9,10},{10,1... | collective-permute-start | bytes 3145736 | tf_op jit(solution)/shard_map/while/body/eval_jaxpr/ppermute | solution.py:56
  391.0 22.6 %collective-permute-start.2 = (s32[2048]{0:T(1024)S(1)}, s32[2048]{0:T(1024)S(1)}, u32[]{:S(2)}, u32[]{:S(2)}) collective-permute-start(s32[2048]{0:T(1024)S(1)} %get-tuple-element.722), channel_id=1, source_target_pairs={{0,1},{1,2},{2,3},{3,4},{4,5},{5,6},{6,7},{7,0},{8,9},{9,10},{10,1... | collective-permute-start | bytes 24584 | tf_op jit(solution)/shard_map/while/body/eval_jaxpr/ppermute | solution.py:58
  418.9 1.6 copy-start.1
Sparse Core Ops, SparseCore 0:
  9.5 92.8 all-gather.2
  439.9 157.9 reduce-scatter.1
where the time goes:
time: 609 us; the launch traced here: 607 us
  waiting for transfers between devices  378 us (62%)
  matrix products  82.7 us (14%)
  local copies, waits for them, and re-layouts  43.5 us (7%)
  starting transfers between devices  33.8 us (6%)
  other arithmetic  33.8 us (6%)
  blocking collectives  20.8 us (3%)
  between operations  13.5 us (2%)
    reduce_scatter x1, waiting for transfers between devices, per_device(): lax.psum_scatter(y_part, 'tp', scatter_dimension=0, tiled=True)  158 us
    ppermute x7, waiting for transfers between devices, kv_step(): seg_cur = lax.ppermute(seg_cur, 'cp', next_perm)  145 us
    all_gather x1, waiting for transfers between devices, per_device(): x_rows = lax.all_gather(x_loc, 'tp', axis=0, tiled=True)  74.1 us
    dot_general x8, matrix products, block_update(): jnp.einsum('qkge,ske->kgqs', q_blk, k_blk, preferred_element_type=jnp.flo...  36.1 us
    while x28, local copies, waits for them, and re-layouts  27.8 us
    all_gather x1, blocking collectives, per_device(): seg_rows = lax.all_gather(seg_loc, 'tp', axis=0, tiled=True)  20.8 us
    ppermute x7, starting transfers between devices, kv_step(): v_cur = lax.ppermute(v_cur, 'cp', next_perm)  17.8 us
    reduce_sum x8, other arithmetic, block_update(): jnp.sum(prob_blk, axis=-1)  17.1 us
  transfers between devices with their start and end apart: 23, of which 9 were waited for; matrix products, arithmetic and copies ran while one was open for 0% of the time, Pallas kernels for 0%

commit v1 on v0

v1 whole, which is shorter than its diff:
```python
import functools

import jax
import jax.numpy as jnp
from jax import lax
from jax.experimental import pallas as pl
from jax.experimental.pallas import tpu as pltpu
from jax.sharding import PartitionSpec as P

NEG_BIG = -1e30
LOG2E = 1.4426950408889634
N_DOCS = 6
SIDE = 4
MESH = pl.DeviceIdType.MESH

BATCHES = (
    ((0, 0, 0), (0, 0, 1)),
    ((0, 1, 0), (0, 3, 0), (1, 0, 1), (3, 0, 1)),
    ((1, 0, 0), (3, 0, 0), (0, 1, 1), (0, 3, 1)),
    ((0, 2, 0), (2, 0, 1), (1, 1, 0), (3, 1, 0), (1, 1, 1), (1, 3, 1)),
    ((1, 3, 0), (3, 3, 0), (3, 1, 1), (3, 3, 1), (2, 0, 0), (0, 2, 1)),
    ((1, 2, 0), (3, 2, 0), (2, 1, 1), (2, 3, 1), (2, 1, 0), (1, 2, 1)),
    ((2, 3, 0), (3, 2, 1), (2, 2, 0), (2, 2, 1)),
)
ORDER = tuple(blk for batch in BATCHES for blk in batch)


def gather_project_kernel(x_hbm, seg_ref, wq_hbm, wk_hbm, wv_hbm, q_ref, kv_hbm, cnt_ref,
                          x_buf, w_buf, kv_own, acc, cnt_mine, cnt_tp, cnt_row, cnt_cp,
                          send_sem, recv_sem, loc_sem, ctp_send, ctp_recv, ccp_send, ccp_recv):
    tp, cp = lax.axis_index("tp"), lax.axis_index("cp")
    n_tp, n_cp = SIDE * SIDE, 2 * SIDE
    z, y = lax.div(tp, SIDE), lax.rem(tp, SIDE)
    x, core = lax.div(cp, 2), lax.rem(cp, 2)
    half_rows = x_buf.shape[3]
    head_dim = q_ref.shape[-1]
    k_tile = 768
    n_used = [0]

    def at(pos, delta):
        return lax.rem(pos + delta, SIDE)

    def remote(src, dst, **device):
        idx = n_used[0]
        n_used[0] += 1
        return pltpu.make_async_remote_copy(src_ref=src, dst_ref=dst, send_sem=send_sem.at[idx], recv_sem=recv_sem.at[idx],
                                            device_id=device, device_id_type=MESH)

    sent = []

    def start(copies):
        for c in copies:
            c.start()
            sent.append(c)
        return copies

    def arrived(copies):
        for c in copies:
            c.wait_recv()

    load_x = pltpu.make_async_copy(x_hbm, x_buf.at[z, y], loc_sem.at[0])
    load_x.start()
    load_w = [pltpu.make_async_copy(w, w_buf.at[i], loc_sem.at[1 + i]) for i, w in enumerate((wq_hbm, wk_hbm, wv_hbm))]
    for c in load_w:
        c.start()
    cnt_mine[...] = (seg_ref[...] < lax.broadcasted_iota(jnp.int32, cnt_mine.shape, 0)).astype(jnp.int32)

    barrier = pltpu.get_barrier_semaphore()
    for d in range(1, n_tp):
        pl.semaphore_signal(barrier, inc=1, device_id={"tp": lax.rem(tp + d, n_tp)}, device_id_type=MESH)
    for d in range(1, n_cp):
        pl.semaphore_signal(barrier, inc=1, device_id={"cp": lax.rem(cp + d, n_cp)}, device_id_type=MESH)
    pl.semaphore_wait(barrier, n_tp - 1 + n_cp - 1)
    load_x.wait()

    def block(fam, b, a, lo=0, n=None):
        rows = pl.ds(lo, half_rows if n is None else n)
        return x_buf.at[b, a, 0, rows] if fam == 0 else x_buf.at[a, b, 1, rows]

    def my(fam):
        return (y, z) if fam == 0 else (z, y)

    def device_a(fam, delta):
        return z * SIDE + at(y, delta) if fam == 0 else at(z, delta) * SIDE + y

    def device_b(fam, delta):
        return device_a(1 - fam, delta)

    def first(fam):
        a, b = my(fam)
        return start([remote(block(fam, b, a), block(fam, b, a), tp=device_a(fam, d)) for d in (1, 3)])

    def first_forward(fam):
        a, b = my(fam)
        up, down = block(fam, b, at(a, 3), 0, half_rows // 2), block(fam, b, at(a, 1), half_rows // 2, half_rows // 2)
        return start([remote(up, up, tp=device_a(fam, 1)), remote(down, down, tp=device_a(fam, 3))])

    def second(fam, da):
        a, b = my(fam)
        src = block(fam, b, at(a, da))
        return start([remote(src, src, tp=device_b(fam, d)) for d in (1, 3)])

    def second_forward(fam, da):
        a, b = my(fam)
        up = block(fam, at(b, 3), at(a, da), 0, half_rows // 2)
        down = block(fam, at(b, 1), at(a, da), half_rows // 2, half_rows // 2)
        return start([remote(up, up, tp=device_b(fam, 1)), remote(down, down, tp=device_b(fam, 3))])

    def both(fn, *args):
        return fn(0, *args) + fn(1, *args)

    def project(i):
        blocks = [(at(z, dz), at(y, dy), h) for dz, dy, h in BATCHES[i]]
        rows = len(blocks) * half_rows
        off = sum(len(b) for b in BATCHES[:i]) * half_rows

        def k_step(kt, _):
            cols = pl.ds(pl.multiple_of(kt * k_tile, k_tile), k_tile)
            lhs = jnp.concatenate([x_buf[bz, by, h, :, cols] for bz, by, h in blocks], axis=0)
            for w in range(3):
                part = jnp.dot(lhs, w_buf[w, cols, :], preferred_element_type=jnp.float32)
                acc[w, :rows, :] = jnp.where(kt == 0, part, acc[w, :rows, :] + part)
            return 0

        lax.fori_loop(0, x_buf.shape[-1] // k_tile, k_step, 0)
        for n, (bz, by, h) in enumerate(blocks):
            q_ref[bz, by, h] = acc[0, n * half_rows:(n + 1) * half_rows, :].astype(jnp.bfloat16)
        kv_own[off:off + rows, :head_dim] = acc[1, :rows, :].astype(jnp.bfloat16)
        kv_own[off:off + rows, head_dim:] = acc[2, :rows, :].astype(jnp.bfloat16)
        return off, rows

    other = x * 2 + 1 - core

    def ring(delta):
        return at(x, delta) * 2 + core

    spans, kv_direct, kv_forward, kv_pair, kv_local = {}, {}, {}, [], []

    def kv_send(i, off, rows):
        span = pl.ds(off, rows)
        spans[i] = (off, rows)
        src, dst = kv_own.at[span], kv_hbm.at[cp, span]
        keep = pltpu.make_async_copy(src, dst, loc_sem.at[4 + i])
        keep.start()
        kv_local.append(keep)
        kv_direct[i] = start([remote(src, dst, cp=ring(1)), remote(src, dst, cp=ring(3))])
        kv_pair.extend(start([remote(src, dst, cp=other)]))

    def kv_relay(i):
        off, rows = spans[i]
        arrived(kv_direct[i])
        up, down = kv_hbm.at[ring(3), pl.ds(off, rows // 2)], kv_hbm.at[ring(1), pl.ds(off + rows // 2, rows // 2)]
        kv_forward[i] = start([remote(up, up, cp=ring(1)), remote(down, down, cp=ring(3))])
        for d in (3, 1):
            ref = kv_hbm.at[ring(d), pl.ds(off, rows)]
            kv_pair.extend(start([remote(ref, ref, cp=other)]))

    def kv_finish(i):
        off, rows = spans[i]
        arrived(kv_forward[i])
        ref = kv_hbm.at[ring(2), pl.ds(off, rows)]
        kv_pair.extend(start([remote(ref, ref, cp=other)]))

    s1 = both(first)
    s2 = {0: both(second, 0)}
    f2 = {}
    ctp = []
    for d in range(1, n_tp):
        c = pltpu.make_async_remote_copy(src_ref=cnt_mine, dst_ref=cnt_tp.at[d - 1], send_sem=ctp_send.at[d - 1], recv_sem=ctp_recv.at[d - 1],
                                         device_id={"tp": lax.rem(tp + d, n_tp)}, device_id_type=MESH)
        c.start()
        ctp.append(c)
    for c in load_w:
        c.wait()
    b0 = project(0)
    arrived(s1)
    f1 = both(first_forward)
    s2[1] = both(second, 1)
    s2[2] = both(second, 3)
    kv_send(0, *b0)
    total = cnt_mine[...]
    for d in range(1, n_tp):
        ctp[d - 1].wait_recv()
        total = total + cnt_tp[d - 1]
    cnt_row[...] = total
    b1 = project(1)
    ccp = []
    for d in range(1, n_cp):
        c = pltpu.make_async_remote_copy(src_ref=cnt_row, dst_ref=cnt_cp.at[d - 1], send_sem=ccp_send.at[d - 1], recv_sem=ccp_recv.at[d - 1],
                                         device_id={"cp": lax.rem(cp + d, n_cp)}, device_id_type=MESH)
        c.start()
        ccp.append(c)
    arrived(s2[0])
    f2[0] = both(second_forward, 0)
    kv_send(1, *b1)
    b2 = project(2)
    arrived(f1)
    s2[3] = both(second, 2)
    kv_relay(0)
    kv_send(2, *b2)
    arrived(s2[1])
    f2[1] = both(second_forward, 1)
    b3 = project(3)
    kv_relay(1)
    kv_finish(0)
    kv_send(3, *b3)
    arrived(s2[2])
    f2[2] = both(second_forward, 3)
    arrived(f2[0])
    b4 = project(4)
    kv_relay(2)
    kv_finish(1)
    kv_send(4, *b4)
    arrived(s2[3])
    f2[3] = both(second_forward, 2)
    arrived(f2[1])
    b5 = project(5)
    kv_relay(3)
    kv_finish(2)
    kv_send(5, *b5)
    arrived(f2[2])
    arrived(f2[3])
    b6 = project(6)
    kv_relay(4)
    kv_send(6, *b6)
    kv_finish(3)
    kv_relay(5)
    kv_finish(4)
    kv_relay(6)
    kv_finish(5)
    kv_finish(6)
    total = cnt_row[...]
    for d in range(1, n_cp):
        ccp[d - 1].wait_recv()
        total = total + cnt_cp[d - 1]
    cnt_ref[...] = total
    arrived(kv_pair)
    for c in sent + ctp + ccp:
        c.wait_send()
    for c in kv_local:
        c.wait()


N_REMOTE = 40 + 7 * 8


def gather_project(x_loc, seg_loc, w_q, w_k, w_v):
    rows, depth = x_loc.shape
    head_dim = w_q.shape[-1]
    half = rows // 2
    n_tp, n_cp = SIDE * SIDE, 2 * SIDE
    most = max(len(b) for b in BATCHES) * half
    any_spec = pl.BlockSpec(memory_space=pl.ANY)
    vmem_spec = pl.BlockSpec(memory_space=pltpu.VMEM)
    dma = pltpu.SemaphoreType.DMA
    q, kv, cnt = pl.pallas_call(
        gather_project_kernel,
        out_shape=(jax.ShapeDtypeStruct((SIDE, SIDE, 2, half, head_dim), jnp.bfloat16),
                   jax.ShapeDtypeStruct((n_cp, n_tp * rows, 2 * head_dim), jnp.bfloat16),
                   jax.ShapeDtypeStruct((8, rows), jnp.int32)),
        in_specs=[any_spec, vmem_spec, any_spec, any_spec, any_spec],
        out_specs=(vmem_spec, any_spec, vmem_spec),
        scratch_shapes=[pltpu.VMEM((SIDE, SIDE, 2, half, depth), jnp.bfloat16), pltpu.VMEM((3, depth, head_dim), jnp.bfloat16),
                        pltpu.VMEM((n_tp * rows, 2 * head_dim), jnp.bfloat16), pltpu.VMEM((3, most, head_dim), jnp.float32),
                        pltpu.VMEM((8, rows), jnp.int32), pltpu.VMEM((n_tp - 1, 8, rows), jnp.int32),
                        pltpu.VMEM((8, rows), jnp.int32), pltpu.VMEM((n_cp - 1, 8, rows), jnp.int32),
                        dma((N_REMOTE,)), dma((N_REMOTE,)), dma((4 + len(BATCHES),)),
                        dma((n_tp - 1,)), dma((n_tp - 1,)), dma((n_cp - 1,)), dma((n_cp - 1,))],
        compiler_params=pltpu.CompilerParams(collective_id=0, has_side_effects=True, vmem_limit_bytes=40 * 2**20),
        cost_estimate=pl.CostEstimate(flops=40 * 10**9, bytes_accessed=30 * 10**6, transcendentals=0),
        name="gather_project",
    )(x_loc.reshape(2, half, depth), seg_loc.reshape(1, rows), w_q, w_k, w_v)
    return q.reshape(n_tp * rows, head_dim), kv.reshape(n_cp * n_tp * rows, 2 * head_dim), jnp.sum(cnt, axis=1)


def flash_kernel(dims, starts, where_am, table, q_ref, kv_hbm, o_ref, kv_buf, m_buf, l_buf, acc_buf, sem):
    n_cp, piece, head_dim, half, tq, tk, nrow = dims
    r, z, y = where_am[0], where_am[1], where_am[2]
    n_pieces = 2 * n_cp
    coef = LOG2E * head_dim ** -0.5
    per_half = piece // half

    def doc_start(pos):
        lo = jnp.zeros_like(pos)
        for d in range(N_DOCS):
            lo = jnp.where(pos >= starts[d], jnp.maximum(lo, starts[d]), lo)
        return lo

    early0, late0 = r * piece, (n_pieces - 1 - r) * piece
    early_lo, late_lo = lax.div(doc_start(early0), piece), lax.div(doc_start(late0), piece)

    def needed(t):
        return ((t >= early_lo) & (t <= r)) | ((t >= late_lo) & (t <= n_pieces - 1 - r))

    def load(t, _):
        @pl.when(needed(t))
        def _():
            late = (t >= n_cp).astype(jnp.int32)
            owner = jnp.where(t >= n_cp, n_pieces - 1 - t, t)

            def one(i, _):
                bz, by, h = late * 2 + lax.div(i, 2 * SIDE), lax.rem(lax.div(i, 2), SIDE), lax.rem(i, 2)
                n = table[lax.rem(bz - z + SIDE, SIDE) * 2 * SIDE + lax.rem(by - y + SIDE, SIDE) * 2 + h]
                pltpu.make_async_copy(kv_hbm.at[pl.ds(pl.multiple_of(owner * 2 * piece + n * half, half), half)],
                                      kv_buf.at[pl.ds(pl.multiple_of(t * piece + i * half, half), half)], sem.at[t]).start()
                return 0

            lax.fori_loop(0, per_half, one, 0)
        return 0

    lax.fori_loop(0, n_pieces, load, 0)

    def settle(t, _):
        @pl.when(needed(t))
        def _():
            ref = kv_buf.at[pl.ds(pl.multiple_of(t * piece, piece), piece)]
            pltpu.make_async_copy(ref, ref, sem.at[t]).wait()
        return 0

    lax.fori_loop(0, r + 1, settle, 0)
    per_piece = piece // tq

    def q_step(qt, _):
        @pl.when(qt == per_piece)
        def _():
            lax.fori_loop(r + 1, n_pieces, settle, 0)
        row0 = pl.multiple_of(qt * tq, tq)
        p0 = jnp.where(qt < per_piece, early0 + row0, late0 + row0 - piece)
        lo0, lo1 = doc_start(p0), doc_start(p0 + tq - 1)
        j_lo, j_hi = lax.div(lo0, tk), lax.div(p0 + tq - 1, tk) + 1
        m_buf[...] = jnp.full_like(m_buf, NEG_BIG)
        l_buf[...] = jnp.zeros_like(l_buf)
        acc_buf[...] = jnp.zeros_like(acc_buf)

        def tile(k0, masked):
            k_blk = kv_buf[pl.ds(k0, tk), :head_dim]
            v_blk = kv_buf[pl.ds(k0, tk), head_dim:]
            for rc in range(tq // nrow):
                rows = pl.ds(rc * nrow, nrow)
                q_blk = q_ref[pl.ds(pl.multiple_of(row0 + rc * nrow, nrow), nrow), :]
                s = lax.dot_general(q_blk, k_blk, (((1,), (1,)), ((), ())), preferred_element_type=jnp.float32)
                if masked:
                    pos_q = p0 + rc * nrow + lax.broadcasted_iota(jnp.int32, (nrow, 128), 0)
                    lo_q = jnp.tile(doc_start(pos_q), (1, tk // 128))
                    pos_q = jnp.tile(pos_q, (1, tk // 128))
                    pos_k = k0 + lax.broadcasted_iota(jnp.int32, (nrow, tk), 1)
                    s = jnp.where((pos_k <= pos_q) & (pos_k >= lo_q), s, NEG_BIG)
                m_old = m_buf[rows, :]
                m_new = jnp.maximum(m_old, jnp.max(s, axis=1, keepdims=True))
                alpha = jnp.exp2((m_old - m_new) * coef)
                p = jnp.exp2((s - jnp.tile(m_new, (1, tk // 128))) * coef)
                l_new = alpha * l_buf[rows, :]
                for c in range(tk // 128):
                    l_new = l_new + p[:, c * 128:(c + 1) * 128]
                l_buf[rows, :] = l_new
                m_buf[rows, :] = m_new
                pv = jnp.dot(p.astype(jnp.bfloat16), v_blk, preferred_element_type=jnp.float32)
                acc_buf[rows, :] = acc_buf[rows, :] * jnp.tile(alpha, (1, head_dim // 128)) + pv

        def kv_step(j, _):
            k0 = pl.multiple_of(j * tk, tk)
            need = (k0 + tk - 1 > p0) | (k0 < lo1)
            pl.when(need)(lambda: tile(k0, True))
            pl.when(jnp.logical_not(need))(lambda: tile(k0, False))
            return 0

        lax.fori_loop(j_lo, j_hi, kv_step, 0)
        l_tot = jnp.sum(l_buf[...], axis=1, keepdims=True)
        o_ref[pl.ds(row0, tq), :] = (acc_buf[...] / l_tot).astype(jnp.bfloat16)
        return 0

    lax.fori_loop(0, 2 * per_piece, q_step, 0)


def flash(starts, where_am, q, kv, half, n_cp, tq=512, tk=1024, nrow=256):
    n_rows, head_dim = q.shape
    piece = n_rows // 2
    dims = (n_cp, piece, head_dim, half, tq, tk, nrow)
    table = [0] * len(ORDER)
    for n, (dz, dy, h) in enumerate(ORDER):
        table[dz * 2 * SIDE + dy * 2 + h] = n
    whole = pl.BlockSpec((n_rows, head_dim), lambda i, *_: (0, 0), pipeline_mode=pl.Buffered(1))
    gs = pltpu.PrefetchScalarGridSpec(
        num_scalar_prefetch=3, grid=(1,), in_specs=[whole, pl.BlockSpec(memory_space=pl.ANY)], out_specs=whole,
        scratch_shapes=[pltpu.VMEM(kv.shape, jnp.bfloat16), pltpu.VMEM((tq, 128), jnp.float32), pltpu.VMEM((tq, 128), jnp.float32),
                        pltpu.VMEM((tq, head_dim), jnp.float32), pltpu.SemaphoreType.DMA((2 * n_cp,))])
    return pl.pallas_call(
        functools.partial(flash_kernel, dims), out_shape=jax.ShapeDtypeStruct((n_rows, head_dim), jnp.bfloat16),
        grid_spec=gs, name="flash", compiler_params=pltpu.CompilerParams(vmem_limit_bytes=40 * 2**20),
        cost_estimate=pl.CostEstimate(flops=20 * 10**9, bytes_accessed=20 * 10**6, transcendentals=0),
    )(starts, where_am, jnp.array(table, jnp.int32), q, kv)


def solution(mesh):
    n_tp, n_cp = mesh.shape["tp"], mesh.shape["cp"]
    pair_perm = [(i, i ^ 1) for i in range(n_cp)]

    def per_device(x_loc, seg_loc, w_q, w_k, w_v, w_o):
        tp, cp = lax.axis_index("tp"), lax.axis_index("cp")
        core = lax.rem(cp, 2)
        rows, depth = x_loc.shape
        head_dim = w_q.shape[-1]
        q, kv, starts = gather_project(x_loc, seg_loc, w_q.reshape(depth, head_dim), w_k.reshape(depth, head_dim), w_v.reshape(depth, head_dim))
        wide = w_o.shape[-1] // 2
        wo_part = lax.dynamic_slice(w_o.reshape(head_dim, 2 * wide), (0, core * wide), (head_dim, wide))
        wo_part, kv = lax.optimization_barrier((wo_part, kv))
        wo_half = lax.all_gather(wo_part, "tp", axis=0, tiled=True)
        where_am = jnp.stack([cp, lax.div(tp, SIDE), lax.rem(tp, SIDE)]).astype(jnp.int32)
        o = flash(starts, where_am, q, kv, rows // 2, n_cp)
        o_heads = lax.all_to_all(o.reshape(n_tp, rows, head_dim), "tp", 0, 0, tiled=False)
        o_rows = o_heads.transpose(1, 0, 2).reshape(rows, n_tp * head_dim)
        o_pair = lax.ppermute(o_rows, "cp", pair_perm)
        both = jnp.concatenate([o_rows, o_pair], axis=0)
        y_both = jnp.dot(both, wo_half, preferred_element_type=jnp.float32).astype(jnp.bfloat16)
        y_mine, y_pair = y_both[:rows], lax.ppermute(y_both[rows:], "cp", pair_perm)
        return jnp.where(core == 0, jnp.concatenate([y_mine, y_pair], axis=1), jnp.concatenate([y_pair, y_mine], axis=1))

    return jax.shard_map(
        per_device, mesh=mesh,
        in_specs=(P(("dp", "cp", "tp"), None), P(("dp", "cp", "tp")), P(None, "tp", None), P(None, "tp", None), P(None, "tp", None), P("tp", None, None)),
        out_specs=P(("dp", "cp", "tp"), None), check_vma=False)
```

time: 609 us -> 238 us (0.39)
  the two profiles are of different devices: /device:TPU:1 before, /device:TPU:7 now
where the time goes in v1:
time: 238 us; the launch traced here: 239 us
  Pallas kernels  145 us (61%)
  blocking collectives  32.9 us (14%)
  waiting for transfers between devices  24.3 us (10%)
  between operations  13.4 us (6%)
  local copies, waits for them, and re-layouts  12 us (5%)
  matrix products  8.33 us (4%)
    pallas_call x1, Pallas kernels, gather_project(): pl.pallas_call(gather_project_kernel, out_shape=(jax.ShapeDtypeStruct((SI...  102 us
    pallas_call x1, Pallas kernels, flash(): pl.pallas_call(functools.partial(flash_kernel, dims), out_shape=jax.Shape...  42.6 us
    all_to_all x1, blocking collectives, per_device(): lax.all_to_all(o.reshape(n_tp, rows, head_dim), 'tp', 0, 0, tiled=False)  32.9 us
    all_gather x1, waiting for transfers between devices, per_device(): wo_half = lax.all_gather(wo_part, 'tp', axis=0, tiled=True)  20.6 us
    unnamed x18, local copies, waits for them, and re-layouts  9.7 us
    dot_general x1, matrix products, per_device(): jnp.dot(both, wo_half, preferred_element_type=jnp.float32)  8.33 us
  transfers between devices with their start and end apart: 3, of which 3 were waited for; matrix products, arithmetic and copies ran while one was open for 1% of the time, Pallas kernels for 18%

profile of v1, /device:TPU:7, one launch (start us, length us, event | category | flops | bytes accessed | tf_op | source)
XLA Modules:
  0.0 238.7 jit_solution(2411705537690314776)
XLA Ops:
  6.5 0.0 copy-start
  6.5 0.0 all-gather.2.cloned.1.call-start
  6.5 1.4 copy-done
  7.9 0.9 dynamic-slice_bitcast_fusion
  8.9 0.0 copy-start.1
  8.9 1.4 copy-done.1
  10.3 0.0 copy-start.2
  10.3 1.4 copy-done.2
  11.7 0.0 copy-start.3
  11.7 1.4 copy-done.3
  13.1 0.0 copy-start.4
  13.1 1.1 copy-done.4
  14.2 0.0 copy-start.5
  14.2 0.7 copy-done.5
  14.9 0.0 copy-start.8
  14.9 102.0 %gather_project.1 = (bf16[4,4,2,64,256]{4,3,2,1,0:T(8,128)(2,1)S(1)}, bf16[8,2048,512]{2,1,0:T(8,128)(2,1)}, s32[8,128]{1,0:T(8,128)S(1)}) custom-call(bf16[2,64,3072]{2,1,0:T(8,128)(2,1)S(1)} %bitcast.21, s32[1,128]{1,0:T(1,128)S(1)} %bitcast.22, bf16[3072,256]{1,0:T(8,128)(2,1)S(1)} %bitcast.18, bf16[3072,256]{1,0:T(8,128)(2,1)S(1)} %bitcast.19, ...), custom_call_target="tpu_custom_call" | custom-call | flops 40000000000 | bytes 30000000 | tf_op jit(solution)/shard_map/gather_project/pallas_call | solution.py:256
  116.9 0.0 copy-start.6
  116.9 1.1 copy-done.6
  118.0 0.0 all-gather.2.cloned.1.call-update
  118.0 0.1 reduce_sum.9.starts
  118.1 0.1 pad_add_fusion.where_am
  118.2 0.0 copy-done.8
  118.2 0.0 copy-start.7
  118.2 1.2 copy-done.7
  119.4 42.6 %flash.1 = bf16[2048,256]{1,0:T(8,128)(2,1)S(1)} custom-call(s32[8]{0:T(128)S(1)} %reduce_sum.9.starts, s32[3]{0:T(128)S(1)} %pad_add_fusion.where_am, s32[32]{0:T(128)S(1)} %copy-done.8, bf16[2048,256]{1,0:T(8,128)(2,1)S(1)} %bitcast.23, bf16[16384,512]{1,0:T(8,128)(2,1)} %bitcast.26), custom_call_target="tpu_custom_call" | custom-call | flops 20000000000 | bytes 20000000 | tf_op jit(solution)/shard_map/flash/pallas_call | solution.py:387
  162.0 1.3 copy.8
  163.3 32.9 %all_to_all.5 = bf16[16,128,256]{1,2,0:T(8,128)(2,1)S(1)} all-to-all(bf16[16,128,256]{1,2,0:T(8,128)(2,1)} %copy.8), channel_id=1, replica_groups=mesh['dp'=1,'tp'=16,'cp'=8] {'tp'}, dimensions={0} | all-to-all | bytes 2097152 | tf_op jit(solution)/shard_map/all_to_all | solution.py:410
  196.2 0.9 collective-permute-start
  197.2 2.3 collective-permute-done
  199.4 20.6 %all-gather.2.cloned.1.call-done = bf16[4096,1536]{1,0:T(8,128)(2,1)} async-done(((bf16[256,1536]{1,0:T(8,128)(2,1)}), bf16[4096,1536]{1,0:T(8,128)(2,1)}) %all-gather.2.cloned.1.call-update) | async-done | bytes 12582928 | tf_op jit(solution)/shard_map/all_gather | solution.py:407
  220.1 8.3 %convolution_convert_fusion = bf16[256,1536]{1,0:T(8,128)(2,1)S(1)} fusion(bf16[4096,1536]{1,0:T(8,128)(2,1)} %all-gather.2.cloned.1.call-done, bf16[128,4096]{0,1:T(8,128)(2,1)} %collective-permute-done, bf16[128,4096]{0,1:T(8,128)(2,1)S(1)} %bitcast.25), kind=kOutput, calls=%fused_computation | convolution fusion | flops 3225812992 | bytes 15466496 | tf_op jit(solution)/shard_map/dot_general | solution.py:414
  228.4 0.1 fusion.4
  228.4 1.0 collective-permute-start.1
  229.5 1.3 collective-permute-done.1
  230.8 1.1 maximum_select_fusion
Async XLA Ops:
  6.5 1.4 copy-start
  6.5 213.5 %all-gather.2.cloned.1.call-start = ((), (), s32[]{:S(2)}) async-start(), calls=%async_computation.1 | async-start | bytes 13369344 | tf_op jit(solution)/shard_map/all_gather | solution.py:407
  8.9 1.4 copy-start.1
  10.3 1.4 copy-start.2
  11.7 1.4 copy-start.3
  13.1 1.1 copy-start.4
  14.2 0.7 copy-start.5
  14.9 103.3 %copy-start.8 = (s32[32]{0:T(128)S(1)}, s32[32]{0:T(128)}, u32[]{:S(2)}) copy-start(s32[32]{0:T(128)} %constant.29.clone.table) | copy-start | bytes 388
  116.9 1.1 copy-start.6
  118.2 1.2 copy-start.7
  196.2 3.2 %collective-permute-start = (bf16[128,4096]{0,1:T(8,128)(2,1)S(1)}, bf16[128,4096]{0,1:T(8,128)(2,1)}, u32[]{:S(2)}, u32[]{:S(2)}) collective-permute-start(bf16[128,4096]{0,1:T(8,128)(2,1)S(1)} %bitcast.24), channel_id=1, source_target_pairs={{0,1},{1,0},{2,3},{3,2},{4,5},{5,4},{6,7},{7,6},{8,9},{9,8},{10,11... | collective-permute-start | bytes 3145736 | tf_op jit(solution)/shard_map/ppermute | solution.py:412
  228.4 2.4 collective-permute-start.1
Sparse Core Ops, SparseCore 0:
  118.1 101.8 all-gather.1

commit v2 on v0

v2 whole, which is shorter than its diff:
```python
import jax
import jax.numpy as jnp
from jax import lax
from jax.experimental import pallas as pl
from jax.experimental.pallas import tpu as pltpu
from jax.sharding import PartitionSpec as P

NEG_BIG = -1e30
LOG2E = 1.4426950408889634
N_DOCS = 6
SIDE = 4
MESH = pl.DeviceIdType.MESH

BATCHES = (
    ((0, 0, 0), (0, 0, 1)),
    ((0, 1, 0), (0, 3, 0), (1, 0, 1), (3, 0, 1)),
    ((1, 0, 0), (3, 0, 0), (0, 1, 1), (0, 3, 1)),
    ((0, 2, 0), (2, 0, 1), (1, 1, 0), (3, 1, 0), (1, 1, 1), (1, 3, 1)),
    ((1, 3, 0), (3, 3, 0), (3, 1, 1), (3, 3, 1), (2, 0, 0), (0, 2, 1)),
    ((1, 2, 0), (3, 2, 0), (2, 1, 1), (2, 3, 1), (2, 1, 0), (1, 2, 1)),
    ((2, 3, 0), (3, 2, 1), (2, 2, 0), (2, 2, 1)),
)
ORDER = tuple(blk for batch in BATCHES for blk in batch)


def attention_kernel(x_hbm, seg_ref, wq_hbm, wk_hbm, wv_hbm, wo_hbm, y_hbm, kv_hbm,
                     x_buf, w_buf, kv_own, acc, q_buf, stage, m_buf, l_buf, o_acc, lo_buf, wo_buf, o_mine, o_all, y_acc, y_out,
                     cnt_mine, cnt_tp, cnt_row, cnt_cp, send_sem, recv_sem, loc_sem, stage_sem):
    tp, cp = lax.axis_index("tp"), lax.axis_index("cp")
    n_tp, n_cp = SIDE * SIDE, 2 * SIDE
    z, y = lax.div(tp, SIDE), lax.rem(tp, SIDE)
    x, core = lax.div(cp, 2), lax.rem(cp, 2)
    other = x * 2 + 1 - core
    half_rows = x_buf.shape[3]
    head_dim = q_buf.shape[-1]
    n_rows = q_buf.shape[0]
    piece = n_rows // 2
    n_pieces = 2 * n_cp
    wide = wo_buf.shape[-1]
    coef = LOG2E * head_dim ** -0.5
    k_tile = 768
    n_used = [0]

    def at(pos, delta):
        return lax.rem(pos + delta, SIDE)

    def remote(src, dst, **device):
        idx = n_used[0]
        n_used[0] += 1
        return pltpu.make_async_remote_copy(src_ref=src, dst_ref=dst, send_sem=send_sem.at[idx], recv_sem=recv_sem.at[idx],
                                            device_id=device, device_id_type=MESH)

    sent = []

    def start(copies):
        for c in copies:
            c.start()
            sent.append(c)
        return copies

    def arrived(copies):
        for c in copies:
            c.wait_recv()

    load_x = pltpu.make_async_copy(x_hbm, x_buf.at[z, y], loc_sem.at[0])
    load_x.start()
    load_w = [pltpu.make_async_copy(w, w_buf.at[i], loc_sem.at[1 + i]) for i, w in enumerate((wq_hbm, wk_hbm, wv_hbm))]
    for c in load_w:
        c.start()
    load_wo = pltpu.make_async_copy(wo_hbm.at[:, :, pl.ds(pl.multiple_of(core * wide, wide), wide)], wo_buf.at[z, y], loc_sem.at[4])
    load_wo.start()
    cnt_mine[...] = (seg_ref[...] < lax.broadcasted_iota(jnp.int32, cnt_mine.shape, 0)).astype(jnp.float32)

    barrier = pltpu.get_barrier_semaphore()
    for d in range(1, n_tp):
        pl.semaphore_signal(barrier, inc=1, device_id={"tp": lax.rem(tp + d, n_tp)}, device_id_type=MESH)
    for d in range(1, n_cp):
        pl.semaphore_signal(barrier, inc=1, device_id={"cp": lax.rem(cp + d, n_cp)}, device_id_type=MESH)
    pl.semaphore_wait(barrier, n_tp - 1 + n_cp - 1)
    load_x.wait()

    def device_a(fam, delta):
        return z * SIDE + at(y, delta) if fam == 0 else at(z, delta) * SIDE + y

    def device_b(fam, delta):
        return device_a(1 - fam, delta)

    class Plane:
        def __init__(self, buf):
            self.buf = buf
            self.rows = buf.shape[3]
            self.s1, self.f1, self.s2, self.f2 = [], [], {}, {}

        def block(self, fam, b, a, part=None):
            half = self.rows // 2
            rows = pl.ds(0, self.rows) if part is None else pl.ds(part * half, half)
            return self.buf.at[b, a, 0, rows] if fam == 0 else self.buf.at[a, b, 1, rows]

        def first(self):
            for fam, (a, b) in enumerate(((y, z), (z, y))):
                src = self.block(fam, b, a)
                self.s1 += start([remote(src, src, tp=device_a(fam, d)) for d in (1, 3)])

        def first_forward(self):
            arrived(self.s1)
            for fam, (a, b) in enumerate(((y, z), (z, y))):
                up, down = self.block(fam, b, at(a, 3), 0), self.block(fam, b, at(a, 1), 1)
                self.f1 += start([remote(up, up, tp=device_a(fam, 1)), remote(down, down, tp=device_a(fam, 3))])

        def second(self, da):
            self.s2[da] = []
            for fam, (a, b) in enumerate(((y, z), (z, y))):
                src = self.block(fam, b, at(a, da))
                self.s2[da] += start([remote(src, src, tp=device_b(fam, d)) for d in (1, 3)])

        def second_forward(self, da):
            arrived(self.s2[da])
            self.f2[da] = []
            for fam, (a, b) in enumerate(((y, z), (z, y))):
                up, down = self.block(fam, at(b, 3), at(a, da), 0), self.block(fam, at(b, 1), at(a, da), 1)
                self.f2[da] += start([remote(up, up, tp=device_b(fam, 1)), remote(down, down, tp=device_b(fam, 3))])

    xs, ws = Plane(x_buf), Plane(wo_buf)

    def project(i):
        blocks = [(at(z, dz), at(y, dy), h) for dz, dy, h in BATCHES[i]]
        rows = len(blocks) * half_rows
        off = sum(len(b) for b in BATCHES[:i]) * half_rows

        def k_step(kt, _):
            cols = pl.ds(pl.multiple_of(kt * k_tile, k_tile), k_tile)
            lhs = jnp.concatenate([x_buf[bz, by, h, :, cols] for bz, by, h in blocks], axis=0)
            for w in range(3):
                part = jnp.dot(lhs, w_buf[w, cols, :], preferred_element_type=jnp.float32)
                acc[w, :rows, :] = jnp.where(kt == 0, part, acc[w, :rows, :] + part)
            return 0

        lax.fori_loop(0, x_buf.shape[-1] // k_tile, k_step, 0)
        for n, (bz, by, h) in enumerate(blocks):
            span = slice(n * half_rows, (n + 1) * half_rows)
            row = pl.ds(pl.multiple_of(((bz * SIDE + by) * 2 + h) * half_rows, half_rows), half_rows)
            q_buf[row, :] = acc[0, span, :].astype(jnp.bfloat16)
            k_new, v_new = acc[1, span, :].astype(jnp.bfloat16), acc[2, span, :].astype(jnp.bfloat16)
            stage[0, row, :head_dim] = k_new
            stage[0, row, head_dim:] = v_new
            kv_own[off + n * half_rows:off + (n + 1) * half_rows, :head_dim] = k_new
            kv_own[off + n * half_rows:off + (n + 1) * half_rows, head_dim:] = v_new
        spans[i] = (off, rows)

    def ring(delta):
        return at(x, delta) * 2 + core

    spans, kv_direct, kv_forward, pair_own, pair_side, pair_far = {}, {}, {}, [], [], []

    def kv_send(i):
        span = pl.ds(*spans[i])
        src, dst = kv_own.at[span], kv_hbm.at[cp, span]
        kv_direct[i] = start([remote(src, dst, cp=ring(1)), remote(src, dst, cp=ring(3))])
        pair_own.extend(start([remote(src, dst, cp=other)]))

    def kv_relay(i):
        off, rows = spans[i]
        arrived(kv_direct[i])
        up, down = kv_hbm.at[ring(3), pl.ds(off, rows // 2)], kv_hbm.at[ring(1), pl.ds(off + rows // 2, rows // 2)]
        kv_forward[i] = start([remote(up, up, cp=ring(1)), remote(down, down, cp=ring(3))])
        for d in (3, 1):
            ref = kv_hbm.at[ring(d), pl.ds(off, rows)]
            pair_side.extend(start([remote(ref, ref, cp=other)]))

    def kv_finish(i):
        arrived(kv_forward[i])
        ref = kv_hbm.at[ring(2), pl.ds(*spans[i])]
        pair_far.extend(start([remote(ref, ref, cp=other)]))

    xs.first()
    xs.second(0)
    ctp = start([remote(cnt_mine, cnt_tp.at[d - 1], tp=lax.rem(tp + d, n_tp)) for d in range(1, n_tp)])
    for c in load_w:
        c.wait()
    project(0)
    xs.first_forward()
    xs.second(1)
    xs.second(3)
    kv_send(0)
    arrived(ctp)
    total = cnt_mine[...]
    for d in range(1, n_tp):
        total = total + cnt_tp[d - 1]
    cnt_row[...] = total
    project(1)
    ccp = start([remote(cnt_row, cnt_cp.at[d - 1], cp=lax.rem(cp + d, n_cp)) for d in range(1, n_cp)])
    xs.second_forward(0)
    kv_send(1)
    project(2)
    arrived(xs.f1)
    xs.second(2)
    kv_relay(0)
    kv_send(2)
    xs.second_forward(1)
    project(3)
    kv_relay(1)
    kv_finish(0)
    kv_send(3)
    xs.second_forward(3)
    arrived(xs.f2[0])
    project(4)
    kv_relay(2)
    kv_finish(1)
    kv_send(4)
    xs.second_forward(2)
    load_wo.wait()
    ws.first()
    ws.second(0)
    arrived(xs.f2[1])
    project(5)
    kv_relay(3)
    kv_finish(2)
    kv_send(5)
    arrived(xs.f2[3])
    arrived(xs.f2[2])
    project(6)
    kv_relay(4)
    kv_send(6)
    kv_finish(3)

    arrived(ccp)
    total = cnt_row[...]
    for d in range(1, n_cp):
        total = total + cnt_cp[d - 1]
    bounds = jnp.sum(total, axis=1, keepdims=True)
    n_part = 256

    def position(row0):
        late = lax.div(row0, piece)
        return (1 - late) * (cp * piece + row0) + late * ((n_pieces - 1 - cp) * piece + row0 - piece)

    def prepare(i, _):
        row0 = pl.multiple_of(i * n_part, n_part)
        pos = (position(row0) + lax.broadcasted_iota(jnp.int32, (n_part, 128), 0)).astype(jnp.float32)
        lo = jnp.zeros_like(pos)
        for d in range(N_DOCS):
            begin = jnp.broadcast_to(bounds[d:d + 1, :], pos.shape)
            lo = jnp.where(pos >= begin, jnp.maximum(lo, begin), lo)
        rows = pl.ds(row0, n_part)
        lo_buf[rows, :] = lo.astype(jnp.int32)
        m_buf[rows, :] = jnp.full((n_part, 128), NEG_BIG, jnp.float32)
        l_buf[rows, :] = jnp.zeros((n_part, 128), jnp.float32)
        o_acc[rows, :] = jnp.zeros((n_part, head_dim), jnp.float32)
        return 0

    lax.fori_loop(0, n_rows // n_part, prepare, 0)

    def attend(slot, row0, key_tile, pos_k0, causal):
        keys = pl.ds(pl.multiple_of(key_tile * piece, piece), piece)
        k_blk = stage[slot, keys, :head_dim]
        v_blk = stage[slot, keys, head_dim:]
        chains = [pl.ds(pl.multiple_of(row0 + c * CHAIN, CHAIN), CHAIN) for c in range(PAIR // CHAIN)]
        lane = lax.broadcasted_iota(jnp.int32, (CHAIN, piece), 1)
        wide_of = lambda v: jnp.tile(v, (1, piece // 128))
        scores = [lax.dot_general(q_buf[rows, :], k_blk, (((1,), (1,)), ((), ())), preferred_element_type=jnp.float32) for rows in chains]
        olds = [(m_buf[rows, :], l_buf[rows, :], o_acc[rows, :], lo_buf[rows, :]) for rows in chains]
        news = []
        for c, (s, (m_old, l_old, o_old, lo)) in enumerate(zip(scores, olds)):
            visible = lane >= wide_of(lo - pos_k0)
            if causal:
                pos_q = position(row0) + c * CHAIN - pos_k0 + lax.broadcasted_iota(jnp.int32, (CHAIN, 128), 0)
                visible = visible & (lane <= wide_of(pos_q))
            s = jnp.where(visible, s, NEG_BIG)
            m_new = jnp.maximum(m_old, jnp.max(s, axis=1, keepdims=True))
            alpha = jnp.exp2((m_old - m_new) * coef)
            p = jnp.exp2((s - wide_of(m_new)) * coef)
            l_new = alpha * l_old
            for i in range(piece // 128):
                l_new = l_new + p[:, i * 128:(i + 1) * 128]
            pv = jnp.dot(p.astype(jnp.bfloat16), v_blk, preferred_element_type=jnp.float32)
            news.append((m_new, l_new, o_old * jnp.tile(alpha, (1, head_dim // 128)) + pv))
        for rows, (m_new, l_new, o_new) in zip(chains, news):
            m_buf[rows, :] = m_new
            l_buf[rows, :] = l_new
            o_acc[rows, :] = o_new

    per_piece = piece // PAIR

    def diagonal(lo, hi):
        def step(u, _):
            key_tile = lax.div(u, 2 * per_piece)
            row0 = (u - key_tile * per_piece) * PAIR
            pos_k0 = (1 - key_tile) * cp * piece + key_tile * (n_pieces - 1 - cp) * piece
            attend(0, row0, key_tile, pos_k0, True)
            return 0
        lax.fori_loop(lo, hi, step, 0)

    def block_of(src, slot):
        earlier = lax.div(cp - src + n_cp - 1, n_cp)

        def step(u, _):
            key_tile = (1 - earlier) * lax.div(u, per_piece)
            row0 = (earlier * u + (1 - earlier) * (per_piece + lax.rem(u, per_piece))) * PAIR
            pos_k0 = (1 - key_tile) * src * piece + key_tile * (n_pieces - 1 - src) * piece
            attend(slot, row0, key_tile, pos_k0, False)
            return 0
        lax.fori_loop(0, 2 * per_piece, step, 0)

    def fetch(src, slot):
        copies = []
        for n, (dz, dy, h) in enumerate(ORDER):
            row = pl.multiple_of(((at(z, dz) * SIDE + at(y, dy)) * 2 + h) * half_rows, half_rows)
            copies.append(pltpu.make_async_copy(kv_hbm.at[src, pl.ds(n * half_rows, half_rows)], stage.at[slot, pl.ds(row, half_rows)], stage_sem.at[slot]))
        for c in copies:
            c.start()
        return pltpu.make_async_copy(kv_hbm.at[src], stage.at[slot], stage_sem.at[slot])

    def landed(whole):
        whole.wait()

    n_diag = 3 * per_piece
    diagonal(0, n_diag // 3)
    kv_relay(5)
    kv_finish(4)
    diagonal(n_diag // 3, 2 * n_diag // 3)
    kv_relay(6)
    kv_finish(5)
    ws.first_forward()
    ws.second(1)
    ws.second(3)
    arrived(pair_own)
    now = fetch(other, 1)
    diagonal(2 * n_diag // 3, n_diag)
    kv_finish(6)
    ws.second_forward(0)

    def near(d, mine):
        return at(x, d) * 2 + (core if mine else 1 - core)

    landed(now)
    now = fetch(near(3, True), 0)
    block_of(other, 1)
    landed(now)
    now = fetch(near(1, True), 1)
    block_of(near(3, True), 0)
    arrived(ws.f1)
    ws.second(2)
    arrived(pair_side)
    landed(now)
    now = fetch(near(3, False), 0)
    block_of(near(1, True), 1)
    ws.second_forward(1)
    landed(now)
    now = fetch(near(1, False), 1)
    block_of(near(3, False), 0)
    ws.second_forward(3)
    landed(now)
    now = fetch(near(2, True), 0)
    block_of(near(1, False), 1)
    arrived(pair_far)
    landed(now)
    now = fetch(near(2, False), 1)
    block_of(near(2, True), 0)
    ws.second_forward(2)
    landed(now)
    block_of(near(2, False), 1)

    def finish(i, _):
        rows = pl.ds(pl.multiple_of(i * 128, 128), 128)
        o_mine[i] = (o_acc[rows, :] / jnp.sum(l_buf[rows, :], axis=1, keepdims=True)).astype(jnp.bfloat16)
        return 0

    lax.fori_loop(0, n_tp, finish, 0)
    turns = (0, 1, 3, 2)
    o_sent = {}
    for dz in turns:
        for dy in turns:
            if dz or dy:
                peer = at(z, dz) * SIDE + at(y, dy)
                o_sent[dz, dy] = start([remote(o_mine.at[peer], o_all.at[tp, 0], tp=peer)])
    o_pair = {(0, 0): start([remote(o_mine.at[tp], o_all.at[tp, 1], cp=other)])}
    o_all[tp, 0] = o_mine[tp]
    for turn, dz in enumerate(turns):
        for dy in turns:
            if dz or dy:
                arrived(o_sent[dz, dy])
                src = at(z, SIDE - dz) * SIDE + at(y, SIDE - dy)
                o_pair[dz, dy] = start([remote(o_all.at[src, 0], o_all.at[src, 1], cp=other)])
    for da in turns:
        arrived(ws.f2[da])
    for turn, dz in enumerate(turns):
        for dy in turns:
            arrived(o_pair[dz, dy])
        zz = at(z, SIDE - dz)

        def column(j, _):
            cols = pl.ds(pl.multiple_of(j * 512, 512), 512)
            lhs = jnp.concatenate([o_all[zz * SIDE + yy].reshape(2 * o_mine.shape[1], head_dim) for yy in range(SIDE)], axis=1)
            rhs = wo_buf[zz, :, :, :, cols].reshape(SIDE * head_dim, 512)
            part = jnp.dot(lhs, rhs, preferred_element_type=jnp.float32)
            y_acc[:, cols] = part if turn == 0 else y_acc[:, cols] + part
            return 0

        lax.fori_loop(0, wide // 512, column, 0)
    y_out[...] = y_acc[...].astype(jnp.bfloat16)
    rows = o_mine.shape[1]
    cols = pl.ds(pl.multiple_of(core * wide, wide), wide)
    keep = pltpu.make_async_copy(y_out.at[pl.ds(0, rows)], y_hbm.at[:, cols], loc_sem.at[5])
    keep.start()
    y_pair = start([remote(y_out.at[pl.ds(rows, rows)], y_hbm.at[:, cols], cp=other)])
    arrived(y_pair)
    keep.wait()
    for c in sent:
        c.wait_send()


N_REMOTE = 2 * 40 + 7 * 8 + 15 + 7 + 15 + 16 + 1
CHAIN = 256
PAIR = 512


def solution(mesh):
    def per_device(x_loc, seg_loc, w_q, w_k, w_v, w_o):
        rows, depth = x_loc.shape
        head_dim = w_q.shape[-1]
        half = rows // 2
        n_tp, n_cp = SIDE * SIDE, 2 * SIDE
        n_rows = n_tp * rows
        wide = w_o.shape[-1] // 2
        most = max(len(b) for b in BATCHES) * half
        hbm = pl.BlockSpec(memory_space=pltpu.HBM)
        f32, bf16 = jnp.float32, jnp.bfloat16
        dma, vmem = pltpu.SemaphoreType.DMA, pltpu.VMEM
        y_loc, _ = pl.pallas_call(
            attention_kernel,
            out_shape=(jax.ShapeDtypeStruct((rows, depth), bf16), jax.ShapeDtypeStruct((n_cp, n_rows, 2 * head_dim), bf16)),
            in_specs=[hbm, pl.BlockSpec(memory_space=vmem), hbm, hbm, hbm, hbm],
            out_specs=(hbm, hbm),
            scratch_shapes=[vmem((SIDE, SIDE, 2, half, depth), bf16), vmem((3, depth, head_dim), bf16),
                            vmem((n_rows, 2 * head_dim), bf16), vmem((3, most, head_dim), f32),
                            vmem((n_rows, head_dim), bf16), vmem((2, n_rows, 2 * head_dim), bf16),
                            vmem((n_rows, 128), f32), vmem((n_rows, 128), f32), vmem((n_rows, head_dim), f32),
                            vmem((n_rows, 128), jnp.int32), vmem((SIDE, SIDE, 2, head_dim // 2, wide), bf16),
                            vmem((n_tp, rows, head_dim), bf16), vmem((n_tp, 2, rows, head_dim), bf16),
                            vmem((2 * rows, wide), f32), vmem((2 * rows, wide), bf16),
                            vmem((8, rows), f32), vmem((n_tp - 1, 8, rows), f32), vmem((8, rows), f32), vmem((n_cp - 1, 8, rows), f32),
                            dma((N_REMOTE,)), dma((N_REMOTE,)), dma((6,)), dma((2,))],
            compiler_params=pltpu.CompilerParams(collective_id=0, has_side_effects=True, vmem_limit_bytes=63 * 2**20),
            cost_estimate=pl.CostEstimate(flops=40 * 10**9, bytes_accessed=30 * 10**6, transcendentals=0),
            name="packed_attention",
        )(x_loc.reshape(2, half, depth), seg_loc.reshape(1, rows), w_q.reshape(depth, head_dim), w_k.reshape(depth, head_dim),
          w_v.reshape(depth, head_dim), w_o.reshape(2, head_dim // 2, 2 * wide))
        return y_loc

    return jax.shard_map(
        per_device, mesh=mesh,
        in_specs=(P(("dp", "cp", "tp"), None), P(("dp", "cp", "tp")), P(None, "tp", None), P(None, "tp", None), P(None, "tp", None), P("tp", None, None)),
        out_specs=P(("dp", "cp", "tp"), None), check_vma=False)
```

time: 609 us -> 172 us (0.28)
  waiting for transfers between devices: 378 us -> 0 us
  Pallas kernels: 0 us -> 169 us
  matrix products: 82.7 us -> 0 us
  local copies, waits for them, and re-layouts: 43.5 us -> 2.06 us
  other arithmetic: 33.8 us -> 0 us
  starting transfers between devices: 33.8 us -> 0 us
  blocking collectives: 20.8 us -> 0 us
  between operations: 13.5 us -> 0.01 us
    pallas_call x0 -> x1, Pallas kernels: none -> 169 us  [per_device(): pl.pallas_call(attention_kernel, out_shape=(jax.ShapeDtypeStruct((rows, d...]
    reduce_scatter x1 -> x0, waiting for transfers between devices: 158 us -> none  [per_device(): lax.psum_scatter(y_part, 'tp', scatter_dimension=0, tiled=True)]
    ppermute x21 -> x0, waiting for transfers between devices: 145 us -> none  [the longest x7 145 us: kv_step(): seg_cur = lax.ppermute(seg_cur, 'cp', next_perm)]
    dot_general x20 -> x0, matrix products: 82.7 us -> none  [the longest x8 36.1 us: block_update(): jnp.einsum('qkge,ske->kgqs', q_blk, k_blk, preferred_element_type=jnp.flo...]
    all_gather x1 -> x0, waiting for transfers between devices: 74.1 us -> none  [per_device(): x_rows = lax.all_gather(x_loc, 'tp', axis=0, tiled=True)]
    ppermute x21 -> x0, starting transfers between devices: 33.7 us -> none  [the longest x7 17.8 us: kv_step(): v_cur = lax.ppermute(v_cur, 'cp', next_perm)]
    while x28 -> x0, local copies, waits for them, and re-layouts: 27.8 us -> none
    all_gather x1 -> x0, blocking collectives: 20.8 us -> none  [per_device(): seg_rows = lax.all_gather(seg_loc, 'tp', axis=0, tiled=True)]
  transfers between devices with their start and end apart: 23 -> 0, of which waited for: 9 -> 0; matrix products, arithmetic and copies ran while one was open for 0% -> 0% of each run, Pallas kernels for 0% -> 0%
where the time goes in v2:
time: 172 us
  Pallas kernels  169 us (98%)
  local copies, waits for them, and re-layouts  2.06 us (1%)
    pallas_call x1, Pallas kernels, per_device(): pl.pallas_call(attention_kernel, out_shape=(jax.ShapeDtypeStruct((rows, d...  169 us

profile of v2, /device:TPU:1, one launch (start us, length us, event | category | flops | bytes accessed | tf_op | source)
XLA Modules:
  0.0 171.5 jit_solution(14407813536537695832)
XLA Ops:
  0.0 169.4 %packed_attention.1 = (bf16[128,3072]{1,0:T(8,128)(2,1)}, bf16[8,2048,512]{2,1,0:T(8,128)(2,1)}) custom-call(bf16[2,64,3072]{2,1,0:T(8,128)(2,1)} %bitcast.10, s32[1,128]{1,0:T(1,128)} %bitcast.11, bf16[3072,256]{1,0:T(8,128)(2,1)} %bitcast.6, bf16[3072,256]{1,0:T(8,128)(2,1)} %bitcast.7, bf16[3072,256]{1,0:T(8,128)(2,1)} %bitcast.8, ...), custom_call_target="tpu_custom_call" | custom-call | flops 40000000000 | bytes 30000000 | tf_op jit(solution)/shard_map/packed_attention/pallas_call | solution.py:429
  169.5 2.1 %copy.8 = bf16[128,3072]{1,0:T(8,128)(2,1)} copy(bf16[128,3072]{1,0:T(8,128)(2,1)} %get-tuple-element.6) | data formatting | bytes 1572864

commit v3 on v2

--- a/solution.py
+++ b/solution.py
@@ -24,7 +24,7 @@
 
 
 def attention_kernel(x_hbm, seg_ref, wq_hbm, wk_hbm, wv_hbm, wo_hbm, y_hbm, kv_hbm,
-                     x_buf, w_buf, kv_own, acc, q_buf, stage, m_buf, l_buf, o_acc, lo_buf, wo_buf, o_mine, o_all, y_acc, y_out,
+                     x_buf, w_buf, kv_own, acc, q_buf, stage, m_buf, l_buf, o_acc, lo_buf, wo_buf, wx_buf, o_mine, o_all, y_acc, y_out,
                      cnt_mine, cnt_tp, cnt_row, cnt_cp, send_sem, recv_sem, loc_sem, stage_sem):
     tp, cp = lax.axis_index("tp"), lax.axis_index("cp")
     n_tp, n_cp = SIDE * SIDE, 2 * SIDE
@@ -36,7 +36,8 @@
     n_rows = q_buf.shape[0]
     piece = n_rows // 2
     n_pieces = 2 * n_cp
-    wide = wo_buf.shape[-1]
+    n_plane, n_quarter = wo_buf.shape[-1], wx_buf.shape[-1]
+    wide = n_plane + SIDE * n_quarter
     coef = LOG2E * head_dim ** -0.5
     k_tile = 768
     n_used = [0]
@@ -67,8 +68,10 @@
     load_w = [pltpu.make_async_copy(w, w_buf.at[i], loc_sem.at[1 + i]) for i, w in enumerate((wq_hbm, wk_hbm, wv_hbm))]
     for c in load_w:
         c.start()
-    load_wo = pltpu.make_async_copy(wo_hbm.at[:, :, pl.ds(pl.multiple_of(core * wide, wide), wide)], wo_buf.at[z, y], loc_sem.at[4])
-    load_wo.start()
+    load_wo = [pltpu.make_async_copy(wo_hbm.at[:, :, pl.ds(pl.multiple_of(core * wide + first, n_quarter), size)], dst, loc_sem.at[4 + i])
+               for i, (first, size, dst) in enumerate(((0, n_plane, wo_buf.at[z, y]), (n_plane + x * n_quarter, n_quarter, wx_buf.at[x, z, y])))]
+    for c in load_wo:
+        c.start()
     cnt_mine[...] = (seg_ref[...] < lax.broadcasted_iota(jnp.int32, cnt_mine.shape, 0)).astype(jnp.float32)
 
     barrier = pltpu.get_barrier_semaphore()
@@ -120,7 +123,7 @@
                 up, down = self.block(fam, at(b, 3), at(a, da), 0), self.block(fam, at(b, 1), at(a, da), 1)
                 self.f2[da] += start([remote(up, up, tp=device_b(fam, 1)), remote(down, down, tp=device_b(fam, 3))])
 
-    xs, ws = Plane(x_buf), Plane(wo_buf)
+    xs, ws, wq = Plane(x_buf), Plane(wo_buf), Plane(wx_buf.at[x])
 
     def project(i):
         blocks = [(at(z, dz), at(y, dy), h) for dz, dy, h in BATCHES[i]]
@@ -178,50 +181,58 @@
     for c in load_w:
         c.wait()
     project(0)
+    kv_send(0)
     xs.first_forward()
     xs.second(1)
     xs.second(3)
-    kv_send(0)
+    project(1)
+    kv_send(1)
     arrived(ctp)
     total = cnt_mine[...]
     for d in range(1, n_tp):
         total = total + cnt_tp[d - 1]
     cnt_row[...] = total
-    project(1)
+    kv_relay(0)
+    xs.second_forward(0)
+    project(2)
+    kv_send(2)
     ccp = start([remote(cnt_row, cnt_cp.at[d - 1], cp=lax.rem(cp + d, n_cp)) for d in range(1, n_cp)])
-    xs.second_forward(0)
-    kv_send(1)
-    project(2)
+    kv_relay(1)
     arrived(xs.f1)
     xs.second(2)
-    kv_relay(0)
-    kv_send(2)
+    kv_finish(0)
     xs.second_forward(1)
     project(3)
-    kv_relay(1)
-    kv_finish(0)
     kv_send(3)
+    kv_relay(2)
+    kv_finish(1)
     xs.second_forward(3)
     arrived(xs.f2[0])
     project(4)
-    kv_relay(2)
-    kv_finish(1)
     kv_send(4)
+    kv_relay(3)
+    kv_finish(2)
     xs.second_forward(2)
-    load_wo.wait()
-    ws.first()
-    ws.second(0)
+    for c in load_wo:
+        c.wait()
+    wq.first()
+    wq.second(0)
     arrived(xs.f2[1])
     project(5)
-    kv_relay(3)
-    kv_finish(2)
     kv_send(5)
+    kv_relay(4)
+    kv_finish(3)
     arrived(xs.f2[3])
     arrived(xs.f2[2])
     project(6)
-    kv_relay(4)
     kv_send(6)
-    kv_finish(3)
+    wq.first_forward()
+    wq.second(1)
+    wq.second(3)
+    ws.first()
+    ws.second(0)
+    kv_relay(5)
+    kv_finish(4)
 
     arrived(ccp)
     total = cnt_row[...]
@@ -314,19 +325,38 @@
         whole.wait()
 
     n_diag = 3 * per_piece
+    wx_direct, wx_forward = [], []
+
+    def wo_along_x():
+        for da in (0, 1, 3, 2):
+            arrived(wq.f2[da])
+        low, high = [wx_buf.at[x, pl.ds(lo, SIDE // 2)] for lo in (0, SIDE // 2)]
+        wx_direct.extend(start([remote(low, low, cp=ring(1)), remote(high, high, cp=ring(3)),
+                                remote(high, high, cp=ring(1)), remote(low, low, cp=ring(3))]))
+
+    def wo_relay_x():
+        arrived(wx_direct[:2])
+        up, down = wx_buf.at[at(x, 3), pl.ds(0, SIDE // 2)], wx_buf.at[at(x, 1), pl.ds(SIDE // 2, SIDE // 2)]
+        wx_forward.extend(start([remote(up, up, cp=ring(1)), remote(down, down, cp=ring(3))]))
+
     diagonal(0, n_diag // 3)
-    kv_relay(5)
-    kv_finish(4)
-    diagonal(n_diag // 3, 2 * n_diag // 3)
+    wq.second_forward(0)
+    arrived(wq.f1)
+    wq.second(2)
     kv_relay(6)
     kv_finish(5)
+    wq.second_forward(1)
+    wq.second_forward(3)
+    diagonal(n_diag // 3, 2 * n_diag // 3)
+    wq.second_forward(2)
     ws.first_forward()
     ws.second(1)
     ws.second(3)
     arrived(pair_own)
     now = fetch(other, 1)
+    kv_finish(6)
     diagonal(2 * n_diag // 3, n_diag)
-    kv_finish(6)
+    wo_along_x()
     ws.second_forward(0)
 
     def near(d, mine):
@@ -335,28 +365,29 @@
     landed(now)
     now = fetch(near(3, True), 0)
     block_of(other, 1)
+    arrived(ws.f1)
+    ws.second(2)
     landed(now)
     now = fetch(near(1, True), 1)
     block_of(near(3, True), 0)
-    arrived(ws.f1)
-    ws.second(2)
+    ws.second_forward(1)
     arrived(pair_side)
     landed(now)
     now = fetch(near(3, False), 0)
     block_of(near(1, True), 1)
-    ws.second_forward(1)
+    wo_relay_x()
+    ws.second_forward(3)
     landed(now)
     now = fetch(near(1, False), 1)
     block_of(near(3, False), 0)
-    ws.second_forward(3)
+    arrived(pair_far)
     landed(now)
     now = fetch(near(2, True), 0)
     block_of(near(1, False), 1)
-    arrived(pair_far)
+    ws.second_forward(2)
     landed(now)
     now = fetch(near(2, False), 1)
     block_of(near(2, True), 0)
-    ws.second_forward(2)
     landed(now)
     block_of(near(2, False), 1)
 
@@ -366,7 +397,7 @@
         return 0
 
     lax.fori_loop(0, n_tp, finish, 0)
-    turns = (0, 1, 3, 2)
+    turns = (2, 1, 3, 0)
     o_sent = {}
     for dz in turns:
         for dy in turns:
@@ -375,32 +406,47 @@
                 o_sent[dz, dy] = start([remote(o_mine.at[peer], o_all.at[tp, 0], tp=peer)])
     o_pair = {(0, 0): start([remote(o_mine.at[tp], o_all.at[tp, 1], cp=other)])}
     o_all[tp, 0] = o_mine[tp]
-    for turn, dz in enumerate(turns):
+    for da in (0, 1, 3, 2):
+        arrived(ws.f2[da])
+    arrived(wx_direct[2:])
+    arrived(wx_forward)
+
+    def pass_on(dz):
         for dy in turns:
             if dz or dy:
                 arrived(o_sent[dz, dy])
                 src = at(z, SIDE - dz) * SIDE + at(y, SIDE - dy)
                 o_pair[dz, dy] = start([remote(o_all.at[src, 0], o_all.at[src, 1], cp=other)])
-    for da in turns:
-        arrived(ws.f2[da])
-    for turn, dz in enumerate(turns):
+
+    def accumulate(turn, dz):
         for dy in turns:
             arrived(o_pair[dz, dy])
         zz = at(z, SIDE - dz)
 
-        def column(j, _):
-            cols = pl.ds(pl.multiple_of(j * 512, 512), 512)
-            lhs = jnp.concatenate([o_all[zz * SIDE + yy].reshape(2 * o_mine.shape[1], head_dim) for yy in range(SIDE)], axis=1)
-            rhs = wo_buf[zz, :, :, :, cols].reshape(SIDE * head_dim, 512)
+        lhs = jnp.concatenate([o_all[zz * SIDE + yy].reshape(2 * o_mine.shape[1], head_dim) for yy in range(SIDE)], axis=1)
+
+        def add(cols, rhs):
             part = jnp.dot(lhs, rhs, preferred_element_type=jnp.float32)
-            y_acc[:, cols] = part if turn == 0 else y_acc[:, cols] + part
-            return 0
-
-        lax.fori_loop(0, wide // 512, column, 0)
-    y_out[...] = y_acc[...].astype(jnp.bfloat16)
+            if turn == 0:
+                y_acc[:, cols] = part
+            elif turn == SIDE - 1:
+                y_out[:, cols] = (y_acc[:, cols] + part).astype(jnp.bfloat16)
+            else:
+                y_acc[:, cols] = y_acc[:, cols] + part
+
+        for j in range(n_plane // 512):
+            cols = pl.ds(j * 512, 512)
+            add(cols, wo_buf[zz, :, :, :, cols].reshape(SIDE * head_dim, 512))
+        add(pl.ds(n_plane, SIDE * n_quarter), jnp.concatenate([wx_buf[xx, zz].reshape(SIDE * head_dim, n_quarter) for xx in range(SIDE)], axis=1))
+
+    pass_on(turns[0])
+    for turn, dz in enumerate(turns):
+        if turn + 1 < SIDE:
+            pass_on(turns[turn + 1])
+        accumulate(turn, dz)
     rows = o_mine.shape[1]
     cols = pl.ds(pl.multiple_of(core * wide, wide), wide)
-    keep = pltpu.make_async_copy(y_out.at[pl.ds(0, rows)], y_hbm.at[:, cols], loc_sem.at[5])
+    keep = pltpu.make_async_copy(y_out.at[pl.ds(0, rows)], y_hbm.at[:, cols], loc_sem.at[6])
     keep.start()
     y_pair = start([remote(y_out.at[pl.ds(rows, rows)], y_hbm.at[:, cols], cp=other)])
     arrived(y_pair)
@@ -409,9 +455,9 @@
         c.wait_send()
 
 
-N_REMOTE = 2 * 40 + 7 * 8 + 15 + 7 + 15 + 16 + 1
-CHAIN = 256
-PAIR = 512
+N_REMOTE = 3 * 40 + 6 + 7 * 8 + 15 + 7 + 15 + 16 + 1
+CHAIN = 512
+PAIR = 1024
 
 
 def solution(mesh):
@@ -435,11 +481,12 @@
                             vmem((n_rows, 2 * head_dim), bf16), vmem((3, most, head_dim), f32),
                             vmem((n_rows, head_dim), bf16), vmem((2, n_rows, 2 * head_dim), bf16),
                             vmem((n_rows, 128), f32), vmem((n_rows, 128), f32), vmem((n_rows, head_dim), f32),
-                            vmem((n_rows, 128), jnp.int32), vmem((SIDE, SIDE, 2, head_dim // 2, wide), bf16),
+                            vmem((n_rows, 128), jnp.int32), vmem((SIDE, SIDE, 2, head_dim // 2, wide // 3 * 2), bf16),
+                            vmem((SIDE, SIDE, SIDE, 2, head_dim // 2, wide // 3 // SIDE), bf16),
                             vmem((n_tp, rows, head_dim), bf16), vmem((n_tp, 2, rows, head_dim), bf16),
                             vmem((2 * rows, wide), f32), vmem((2 * rows, wide), bf16),
                             vmem((8, rows), f32), vmem((n_tp - 1, 8, rows), f32), vmem((8, rows), f32), vmem((n_cp - 1, 8, rows), f32),
-                            dma((N_REMOTE,)), dma((N_REMOTE,)), dma((6,)), dma((2,))],
+                            dma((N_REMOTE,)), dma((N_REMOTE,)), dma((7,)), dma((2,))],
             compiler_params=pltpu.CompilerParams(collective_id=0, has_side_effects=True, vmem_limit_bytes=63 * 2**20),
             cost_estimate=pl.CostEstimate(flops=40 * 10**9, bytes_accessed=30 * 10**6, transcendentals=0),
             name="packed_attention",

time: 172 us -> 156 us (0.907)
  Pallas kernels: 169 us -> 154 us
    pallas_call x1, Pallas kernels: 169 us -> 154 us  [per_device(): pl.pallas_call(attention_kernel, out_shape=(jax.ShapeDtypeStruct((rows, d...]
where the time goes in v3:
time: 156 us
  Pallas kernels  154 us (99%)
  local copies, waits for them, and re-layouts  2.06 us (1%)
    pallas_call x1, Pallas kernels, per_device(): pl.pallas_call(attention_kernel, out_shape=(jax.ShapeDtypeStruct((rows, d...  154 us

profile of v3, /device:TPU:1, one launch (start us, length us, event | category | flops | bytes accessed | tf_op | source)
XLA Modules:
  0.0 155.8 jit_solution(16046036982977382853)
XLA Ops:
  0.0 153.7 %packed_attention.1 = (bf16[128,3072]{1,0:T(8,128)(2,1)}, bf16[8,2048,512]{2,1,0:T(8,128)(2,1)}) custom-call(bf16[2,64,3072]{2,1,0:T(8,128)(2,1)} %bitcast.10, s32[1,128]{1,0:T(1,128)} %bitcast.11, bf16[3072,256]{1,0:T(8,128)(2,1)} %bitcast.6, bf16[3072,256]{1,0:T(8,128)(2,1)} %bitcast.7, bf16[3072,256]{1,0:T(8,128)(2,1)} %bitcast.8, ...), custom_call_target="tpu_custom_call" | custom-call | flops 40000000000 | bytes 30000000 | tf_op jit(solution)/shard_map/packed_attention/pallas_call | solution.py:475
  153.7 2.1 %copy.8 = bf16[128,3072]{1,0:T(8,128)(2,1)} copy(bf16[128,3072]{1,0:T(8,128)(2,1)} %get-tuple-element.6) | data formatting | bytes 1572864

commit v4 on v3

--- a/solution.py
+++ b/solution.py
@@ -301,7 +301,7 @@
             return 0
         lax.fori_loop(lo, hi, step, 0)
 
-    def block_of(src, slot):
+    def block_of(src, slot, lo=0, hi=None):
         earlier = lax.div(cp - src + n_cp - 1, n_cp)
 
         def step(u, _):
@@ -310,7 +310,7 @@
             pos_k0 = (1 - key_tile) * src * piece + key_tile * (n_pieces - 1 - src) * piece
             attend(slot, row0, key_tile, pos_k0, False)
             return 0
-        lax.fori_loop(0, 2 * per_piece, step, 0)
+        lax.fori_loop(lo, 2 * per_piece if hi is None else hi, step, 0)
 
     def fetch(src, slot):
         copies = []
@@ -387,23 +387,38 @@
     ws.second_forward(2)
     landed(now)
     now = fetch(near(2, False), 1)
-    block_of(near(2, True), 0)
-    landed(now)
-    block_of(near(2, False), 1)
+    block_of(near(2, True), 0, 0, per_piece)
+    landed(now)
+    block_of(near(2, False), 1, 0, per_piece)
 
     def finish(i, _):
         rows = pl.ds(pl.multiple_of(i * 128, 128), 128)
         o_mine[i] = (o_acc[rows, :] / jnp.sum(l_buf[rows, :], axis=1, keepdims=True)).astype(jnp.bfloat16)
         return 0
 
-    lax.fori_loop(0, n_tp, finish, 0)
     turns = (2, 1, 3, 0)
     o_sent = {}
     for dz in turns:
         for dy in turns:
             if dz or dy:
                 peer = at(z, dz) * SIDE + at(y, dy)
-                o_sent[dz, dy] = start([remote(o_mine.at[peer], o_all.at[tp, 0], tp=peer)])
+                o_sent[dz, dy] = [remote(o_mine.at[peer], o_all.at[tp, 0], tp=peer)]
+                sent.extend(o_sent[dz, dy])
+
+    def hand_out(late):
+        for dz in turns:
+            @pl.when(lax.div(at(z, dz), SIDE // 2) == late)
+            def _():
+                for dy in turns:
+                    if dz or dy:
+                        o_sent[dz, dy][0].start()
+
+    lax.fori_loop(0, n_tp // 2, finish, 0)
+    hand_out(0)
+    block_of(near(2, True), 0, per_piece, 2 * per_piece)
+    block_of(near(2, False), 1, per_piece, 2 * per_piece)
+    lax.fori_loop(n_tp // 2, n_tp, finish, 0)
+    hand_out(1)
     o_pair = {(0, 0): start([remote(o_mine.at[tp], o_all.at[tp, 1], cp=other)])}
     o_all[tp, 0] = o_mine[tp]
     for da in (0, 1, 3, 2):

time: 156 us -> 153 us (0.981); the launches traced: 156 us -> 151 us
  Pallas kernels: 154 us -> 149 us
    pallas_call x1, Pallas kernels: 154 us -> 149 us  [per_device(): pl.pallas_call(attention_kernel, out_shape=(jax.ShapeDtypeStruct((rows, d...]
where the time goes in v4:
time: 153 us; the launch traced here: 151 us
  Pallas kernels  149 us (97%)
  local copies, waits for them, and re-layouts  2.06 us (1%)
    pallas_call x1, Pallas kernels, per_device(): pl.pallas_call(attention_kernel, out_shape=(jax.ShapeDtypeStruct((rows, d...  149 us

profile of v4, /device:TPU:1, one launch (start us, length us, event | category | flops | bytes accessed | tf_op | source)
XLA Modules:
  0.0 150.9 jit_solution(13021887815524537237)
XLA Ops:
  0.0 148.8 %packed_attention.1 = (bf16[128,3072]{1,0:T(8,128)(2,1)}, bf16[8,2048,512]{2,1,0:T(8,128)(2,1)}) custom-call(bf16[2,64,3072]{2,1,0:T(8,128)(2,1)} %bitcast.10, s32[1,128]{1,0:T(1,128)} %bitcast.11, bf16[3072,256]{1,0:T(8,128)(2,1)} %bitcast.6, bf16[3072,256]{1,0:T(8,128)(2,1)} %bitcast.7, bf16[3072,256]{1,0:T(8,128)(2,1)} %bitcast.8, ...), custom_call_target="tpu_custom_call" | custom-call | flops 40000000000 | bytes 30000000 | tf_op jit(solution)/shard_map/packed_attention/pallas_call | solution.py:490
  148.8 2.1 %copy.8 = bf16[128,3072]{1,0:T(8,128)(2,1)} copy(bf16[128,3072]{1,0:T(8,128)(2,1)} %get-tuple-element.6) | data formatting | bytes 1572864
